TPU v7x, 8 devices: a whole 2x2x1 slice. The times are simulated.
8 devices in a mesh: dp: 8 (over z, y, x, core).
Axes of the slice: x: 2, y: 2, z: 1, core: 2. Of those that a mesh axis runs over, the one named last changes fastest.
Arguments:
- g_mat: bfloat16 [8, 14155776], P('dp')
- g_vec: bfloat16 [8, 19968], P('dp')
- p_mat: float32 [14155776], P('dp')
- m_mat: float32 [14155776], P('dp')
- v_mat: float32 [14155776], P('dp')
- p_vec: float32 [19968], replicated
- m_vec: float32 [19968], replicated
- v_vec: float32 [19968], replicated
- learn_rate: float32 [], replicated
Outputs:
- output 1: float32 [14155776], P('dp')
- output 2: float32 [14155776], P('dp')
- output 3: float32 [14155776], P('dp')
- output 4: float32 [19968], replicated
- output 5: float32 [19968], replicated
- output 6: float32 [19968], replicated
- output 7: bfloat16 [14155776], replicated
All inputs are finite; a program needn't handle non-finite values.
Results may differ from a plain program's by a relative error of at most 0.001.
Values are sent between devices in bfloat16 or wider.
A program may use at most 1 GiB of HBM per device.

v0:
```python
import jax
import jax.numpy as jnp
from jax import lax
from jax.sharding import PartitionSpec as P

STEP = 10
ADAM_BETA1 = 0.9
ADAM_BETA2 = 0.98
ADAM_EPS = 1e-8
WEIGHT_DECAY = 0.01
MAX_NORM = 1.0
NORM_EPS = 1e-6
BIAS_ONE = 1.0 - ADAM_BETA1 ** STEP
BIAS_TWO = 1.0 - ADAM_BETA2 ** STEP


def adam_update(grad_vals, param_vals, moment_one, moment_two, learn_rate, decay_rate):
    new_one = ADAM_BETA1 * moment_one + (1.0 - ADAM_BETA1) * grad_vals
    new_two = ADAM_BETA2 * moment_two + (1.0 - ADAM_BETA2) * grad_vals * grad_vals
    direction = (new_one / BIAS_ONE) / (jnp.sqrt(new_two / BIAS_TWO) + ADAM_EPS)
    return param_vals - learn_rate * (direction + decay_rate * param_vals), new_one, new_two


def solution(mesh):
    axis_name = mesh.axis_names[0]
    group_size = mesh.shape[axis_name]

    def local_step(g_mat, g_vec, p_mat, m_mat, v_mat, p_vec, m_vec, v_vec, learn_rate):
        send_rows = g_mat.reshape(group_size, -1)
        recv_rows = lax.all_to_all(send_rows, axis_name, 0, 0, tiled=True)
        grad_mat = jnp.sum(recv_rows.astype(jnp.float32), axis=0) / group_size
        grad_vec = lax.psum(g_vec[0].astype(jnp.float32), axis_name) / group_size
        norm_sq = lax.psum(jnp.sum(grad_mat * grad_mat), axis_name) + jnp.sum(grad_vec * grad_vec)
        clip_scale = jnp.minimum(1.0, MAX_NORM / (jnp.sqrt(norm_sq) + NORM_EPS))
        new_p_mat, new_m_mat, new_v_mat = adam_update(grad_mat * clip_scale, p_mat, m_mat, v_mat, learn_rate, WEIGHT_DECAY)
        new_p_vec, new_m_vec, new_v_vec = adam_update(grad_vec * clip_scale, p_vec, m_vec, v_vec, learn_rate, 0.0)
        full_params = lax.all_gather(new_p_mat.astype(jnp.bfloat16), axis_name, tiled=True)
        return new_p_mat, new_m_mat, new_v_mat, new_p_vec, new_m_vec, new_v_vec, full_params

    return jax.shard_map(
        local_step,
        mesh=mesh,
        in_specs=(P(axis_name, None), P(axis_name, None), P(axis_name), P(axis_name), P(axis_name), P(), P(), P(), P()),
        out_specs=(P(axis_name), P(axis_name), P(axis_name), P(), P(), P(), P()),
        check_vma=False,
    )
```

profile of v0, /device:TPU:0, one launch (start us, length us, event | category | flops | bytes accessed | tf_op | source)
XLA Modules:
  0.0 989.7 jit_solution(5980367169978962879)
XLA Ops:
  7.2 0.5 broadcast.9
  7.7 167.0 %reduce.3 = bf16[8,1769472]{1,0:T(8,128)(2,1)} reduce(bf16[8,1,1769472]{2,1,0:T(2,128)(2,1)} %bitcast.1, bf16[]{:T(256)} %broadcast.9), dimensions={1}, to_apply=%bitcast.reduce_sub_computation | reduce | bytes 56623104 | tf_op jit(solution)/shard_map/all_to_all | solution.py:30
  174.6 147.2 %reshape.23 = bf16[8,2,884736]{2,1,0:T(2,128)(2,1)} reshape(bf16[8,1769472]{1,0:T(8,128)(2,1)} %reduce.3) | data formatting | bytes 56623104
  321.8 0.0 copy-start.4
  321.8 5.5 all-to-all-start
  327.4 0.0 all-reduce.2.cloned.1.call-start
  327.4 0.0 copy-done.4
  327.4 0.8 convert_reduce_fusion.1
  328.3 0.0 all-reduce.2.cloned.1.call-update
  328.3 0.0 all-gather.2.cloned.1.call-start
  329.0 308.6 %all-to-all-done = bf16[8,2,884736]{2,1,0:T(2,128)(2,1)} async-done(((bf16[8,2,884736]{2,1,0:T(2,128)(2,1)}), bf16[8,2,884736]{2,1,0:T(2,128)(2,1)}, u32[]{:S(2)}, u32[]{:S(2)}) %all-to-all-start) | async-done | bytes 28311584 | tf_op jit(solution)/shard_map/all_to_all | solution.py:30
  637.6 62.6 %reshape.24 = bf16[8,1,1769472]{2,1,0:T(2,128)(2,1)} reshape(bf16[8,2,884736]{2,1,0:T(2,128)(2,1)} %all-to-all-done) | data formatting | bytes 56623104
  700.2 78.6 %convert_reduce_fusion = f32[1769472]{0:T(1024)} fusion(bf16[8,1,1769472]{2,1,0:T(2,128)(2,1)} %reshape.24), kind=kLoop, calls=%fused_computation | loop fusion | flops 26542080 | bytes 35389440 | tf_op jit(solution)/shard_map/reduce_sum | solution.py:31
  778.9 4.6 multiply_reduce_fusion
  783.5 0.0 all-reduce.2.cloned.1.call-done
  783.5 1.5 multiply_reduce_fusion.1
  785.0 22.4 %psum.14 = f32[]{:T(128)} all-reduce(f32[]{:T(128)} %multiply_reduce_fusion), channel_id=1, replica_groups=mesh['dp'=8] {'dp'}, use_global_device_ids=true, to_apply=%region_2.0 | all-reduce | flops 1 | bytes 8 | tf_op jit(solution)/shard_map/psum | solution.py:33
  808.8 0.0 copy-start
  808.8 0.0 copy-start.1
  808.8 0.0 copy-start.2
  808.8 0.0 copy-start.3
  808.8 20.1 %fusion.2 = (bf16[1769472]{0:T(1024)(128)(2,1)}, f32[1769472]{0:T(1024)}, f32[1769472]{0:T(1024)}, f32[1769472]{0:T(1024)}) fusion(f32[1769472]{0:T(1024)} %param.11, f32[]{:T(128)S(6)} %copy.18, f32[1769472]{0:T(1024)} %convert_reduce_fusion, f32[]{:T(128)S(6)} %mul.103, f32[1769472]{0:T(1024)} %param.12, f32[1769472]{0:T(1024)} %param.13), kind=kLoop, calls=%fused_computation.12 | loop fusion | flops 30081024 | bytes 53084168 | tf_op jit(solution)/shard_map/convert_element_type | solution.py:37
  828.9 0.0 all-gather.2.cloned.1.call-update
  828.9 0.0 copy-done
  828.9 0.0 copy-done.1
  828.9 0.0 copy-done.2
  829.0 0.0 copy-done.3
  829.0 0.7 multiply_subtract_fusion.1
  829.7 133.4 %all-gather.2.cloned.1.call-done = bf16[14155776]{0:T(1024)(128)(2,1)} async-done(((bf16[1769472]{0:T(1024)(128)(2,1)}), bf16[14155776]{0:T(1024)(128)(2,1)}) %all-gather.2.cloned.1.call-update) | async-done | bytes 28311568 | tf_op jit(solution)/shard_map/all_gather | solution.py:37
  963.1 19.4 %copy.19 = bf16[14155776]{0:T(1024)(128)(2,1)} copy(bf16[14155776]{0:T(1024)(128)(2,1)} %all-gather.2.cloned.1.call-done) | data formatting | bytes 56623104
Async XLA Ops:
  321.8 5.6 copy-start.4
  321.8 315.8 %all-to-all-start = ((bf16[8,2,884736]{2,1,0:T(2,128)(2,1)}), bf16[8,2,884736]{2,1,0:T(2,128)(2,1)}, u32[]{:S(2)}, u32[]{:S(2)}) async-start(bf16[8,2,884736]{2,1,0:T(2,128)(2,1)} %reshape.23), calls=%async_computation | async-start | bytes 56623104 | tf_op jit(solution)/shard_map/all_to_all | solution.py:30
  327.4 456.1 %all-reduce.2.cloned.1.call-start = ((), (), s32[]{:S(2)}) async-start(), calls=%async_computation.1 | async-start | bytes 163840 | tf_op jit(solution)/shard_map/psum | solution.py:32
  328.3 634.8 %all-gather.2.cloned.1.call-start = ((), (), s32[]{:S(2)}) async-start(), calls=%async_computation.2 | async-start | bytes 31850496 | tf_op jit(solution)/shard_map/all_gather | solution.py:37
  808.8 20.2 %copy-start = (f32[19968]{0:T(1024)S(1)}, f32[19968]{0:T(1024)}, u32[]{:S(2)}) copy-start(f32[19968]{0:T(1024)} %all-reduce.2.cloned.1.call-done) | copy-start | bytes 239620
  808.8 20.2 %copy-start.1 = (f32[19968]{0:T(1024)S(1)}, f32[19968]{0:T(1024)}, u32[]{:S(2)}) copy-start(f32[19968]{0:T(1024)} %param.14) | copy-start | bytes 239620
  808.8 20.2 %copy-start.2 = (f32[19968]{0:T(1024)S(1)}, f32[19968]{0:T(1024)}, u32[]{:S(2)}) copy-start(f32[19968]{0:T(1024)} %param.15) | copy-start | bytes 239620
  808.8 20.2 %copy-start.3 = (f32[19968]{0:T(1024)S(1)}, f32[19968]{0:T(1024)}, u32[]{:S(2)}) copy-start(f32[19968]{0:T(1024)} %param.16) | copy-start | bytes 239620
Sparse Core Ops, SparseCore 0:
  331.8 193.3 all-reduce.1
  829.0 133.9 all-gather.1
where the time goes:
time: 1000 us; the launch traced here: 990 us
  waiting for transfers between devices  442 us (44%)
  other arithmetic  273 us (27%)
  local copies, waits for them, and re-layouts  230 us (23%)
  blocking collectives  22.4 us (2%)
  between operations  16.6 us (2%)
    all_to_all x1, waiting for transfers between devices, local_step(): recv_rows = lax.all_to_all(send_rows, axis_name, 0, 0, tiled=True)  309 us
    unnamed x13, local copies, waits for them, and re-layouts  229 us
    all_to_all x1, other arithmetic, local_step(): recv_rows = lax.all_to_all(send_rows, axis_name, 0, 0, tiled=True)  167 us
    all_gather x1, waiting for transfers between devices, local_step(): lax.all_gather(new_p_mat.astype(jnp.bfloat16), axis_name, tiled=True)  133 us
    reduce_sum x1, other arithmetic, local_step(): grad_mat = jnp.sum(recv_rows.astype(jnp.float32), axis=0) / group_size  78.6 us
    psum x1, blocking collectives, local_step(): lax.psum(jnp.sum(grad_mat * grad_mat), axis_name)  22.4 us
    convert_element_type x1, other arithmetic, local_step(): new_p_mat.astype(jnp.bfloat16)  20.1 us
  transfers between devices with their start and end apart: 3, of which 2 were waited for; matrix products, arithmetic and copies ran while one was open for 15% of the time, Pallas kernels for 0%

commit v1 on v0

v1 whole, which is shorter than its diff:
```python
import functools

import jax
import jax.numpy as jnp
from jax import lax
from jax.experimental import pallas as pl
from jax.experimental.pallas import tpu as pltpu
from jax.sharding import PartitionSpec as P

STEP = 10
ADAM_BETA1 = 0.9
ADAM_BETA2 = 0.98
ADAM_EPS = 1e-8
WEIGHT_DECAY = 0.01
MAX_NORM = 1.0
NORM_EPS = 1e-6
BIAS_ONE = 1.0 - ADAM_BETA1 ** STEP
BIAS_TWO = 1.0 - ADAM_BETA2 ** STEP

LANES = 128
N_DEV = 8
NC = 18
NRAW = 8
LAG = 2
VROWS = 80
MESH = pl.DeviceIdType.MESH
F32 = jnp.float32
BF16 = jnp.bfloat16


def adam_update(grad_vals, param_vals, moment_one, moment_two, learn_rate, decay_rate):
    new_one = ADAM_BETA1 * moment_one + (1.0 - ADAM_BETA1) * grad_vals
    new_two = ADAM_BETA2 * moment_two + (1.0 - ADAM_BETA2) * grad_vals * grad_vals
    direction = (new_one / BIAS_ONE) / (jnp.sqrt(new_two / BIAS_TWO) + ADAM_EPS)
    return param_vals - learn_rate * (direction + decay_rate * param_vals), new_one, new_two


def flip(device, mask):
    for bit in (1, 2, 4):
        if mask & bit:
            device = device + bit - 2 * bit * lax.rem(lax.div(device, bit), 2)
    return device


def step_kernel(
    half, rc, n_vec,
    g_hbm, gv_hbm, p_hbm, m_hbm, v_hbm, pv_ref, mv_ref, vv_ref, lr_ref,
    big, p_ref, m_ref, v_ref, pv_out, mv_out, vv_out,
    fin, raw, pk, rel, acc, norms, vraw, vpk, vland, vs1, vlx, vs2, vly, vfull,
    raw_sem, send_sem, rel_sem, rs, st_sem, ns_sem, nr_sem, vs_sem, vr_sem, ag_sem,
):
    piece_rows = 2 * half
    me = lax.axis_index("dp")
    core = lax.rem(me, 2)
    peer = {mask: flip(me, mask) for mask in range(1, N_DEV)}

    def remote(src, dst, ssem, rsem, mask):
        return pltpu.make_async_remote_copy(
            src_ref=src, dst_ref=dst, send_sem=ssem, recv_sem=rsem,
            device_id=(peer[mask],), device_id_type=MESH,
        )

    def rows(first, count, align=16):
        return pl.ds(pl.multiple_of(first, align), count)

    blocks = []
    for j in (0, 1):
        for h in (0, 1):
            via = (4, 2)[h]
            blocks.append(("send", h, 6 ^ j, via ^ j, h * 3 + j))
    for h in (0, 1):
        blocks.append(("send", h, (2, 4)[h] ^ 1, 1, h * 3 + 2))
        blocks.append(("own", h, (2, 4)[h], None, 14 + h))
    for j in (0, 1):
        for h in (0, 1):
            via = (4, 2)[h]
            blocks.append(("send", h, via ^ j, via ^ j, 6 + h * 3 + j))
    for h in (0, 1):
        blocks.append(("send", h, 1, 1, 6 + h * 3 + 2))
        blocks.append(("own", h, 0, None, 12 + h))
    n_blocks = len(blocks)
    send_slot = {}
    for b, block in enumerate(blocks):
        if block[0] == "send":
            send_slot[b] = len(send_slot)

    def raw_copy(b, c):
        _, h, mask, _, _ = blocks[b]
        piece = flip(me, mask) if mask else me
        start = (piece * piece_rows + h * half + c * rc) * LANES
        return pltpu.make_async_copy(
            g_hbm.at[:, pl.ds(pl.multiple_of(start, 2048), rc * LANES)],
            raw.at[b % NRAW], raw_sem.at[b % NRAW],
        )

    def block_copy(b, c):
        _, h, _, dest, slot = blocks[b]
        s = send_slot[b]
        par = lax.rem(c, 2)
        return remote(
            pk.at[par, s], big.at[rows(slot * half + c * rc, rc)],
            send_sem.at[par, s], rs.at[slot, c], dest,
        )

    def landed(slot, c):
        ref = big.at[rows(slot * half + c * rc, rc)]
        return remote(ref, ref, send_sem.at[0, 0], rs.at[slot, c], 1)

    def rel_copy(h, c):
        par = lax.rem(c, 2)
        return remote(
            rel.at[par, h], fin.at[rows(h * half + c * rc, rc)],
            rel_sem.at[par, h], rs.at[12 + h, c], (2, 4)[h],
        )

    state_copies = [
        pltpu.make_async_copy(src, dst, st_sem.at[i])
        for i, (src, dst) in enumerate(((p_hbm, p_ref), (m_hbm, m_ref), (v_hbm, v_ref)))
    ]
    vraw_copy = pltpu.make_async_copy(gv_hbm, vraw.at[:, pl.ds(0, n_vec)], st_sem.at[3])

    barrier = pltpu.get_barrier_semaphore()
    for mask in range(1, N_DEV):
        pl.semaphore_signal(barrier, inc=1, device_id=(peer[mask],), device_id_type=MESH)
    for b in range(NRAW):
        raw_copy(b, 0).start()
    vraw[:, pl.ds(n_vec // 1024 * 1024, 2 * VROWS * LANES - n_vec // 1024 * 1024)] = jnp.zeros(
        (1, 2 * VROWS * LANES - n_vec // 1024 * 1024), BF16)
    acc[...] = jnp.zeros_like(acc)
    pl.semaphore_wait(barrier, N_DEV - 1)

    step_rows = 64

    def pack_rows(src, dst, first):
        def body(i, _):
            vals = src[:, pl.ds(pl.multiple_of(i * step_rows * LANES, 2048), step_rows * LANES)]
            dst[rows(first + i * step_rows, step_rows), :] = (
                vals.astype(F32).reshape(step_rows, LANES).astype(BF16))
            return 0
        lax.fori_loop(0, rc // step_rows, body, 0)

    def send_chunk(c):
        par = lax.rem(c, 2)
        waiting = None
        for b, (kind, h, mask, dest, slot) in enumerate(blocks):
            raw_copy(b, c).wait()
            if kind == "send":
                @pl.when(c >= 2)
                def _():
                    block_copy(b, c - 2).wait_send()
                pack_rows(raw.at[b % NRAW], pk.at[par, send_slot[b]], 0)
            else:
                pack_rows(raw.at[b % NRAW], big, slot * half + c * rc)
            if b + NRAW < n_blocks:
                raw_copy(b + NRAW, c).start()
            else:
                @pl.when(c + 1 < NC)
                def _():
                    raw_copy(b + NRAW - n_blocks, c + 1).start()
            if waiting is not None:
                block_copy(waiting, c).start()
            waiting = b if kind == "send" else None
        if waiting is not None:
            block_copy(waiting, c).start()

    sum_rows = 32

    def relay_chunk(c):
        par = lax.rem(c, 2)
        for h in (0, 1):
            for j in range(3):
                landed(h * 3 + j, c).wait_recv()

            @pl.when(c >= 2)
            def _():
                rel_copy(h, c - 2).wait_send()

            def body(i, _):
                at = c * rc + i * sum_rows
                total = big[rows((14 + h) * half + at, sum_rows), :].astype(F32)
                for j in (2, 0, 1):
                    total = total + big[rows((h * 3 + j) * half + at, sum_rows), :].astype(F32)
                rel[par, h, rows(i * sum_rows, sum_rows), :] = total
                return 0
            lax.fori_loop(0, rc // sum_rows, body, 0)
        for h in (0, 1):
            rel_copy(h, c).start()

    def final_chunk(c):
        for h in (0, 1):
            for j in range(3):
                landed(6 + h * 3 + j, c).wait_recv()
            rel_copy(h, c).wait_recv()

            def body(i, sq):
                at = c * rc + i * sum_rows
                total = big[rows((12 + h) * half + at, sum_rows), :].astype(F32)
                for j in (2, 0, 1):
                    total = total + big[rows((6 + h * 3 + j) * half + at, sum_rows), :].astype(F32)
                total = total + fin[rows(h * half + at, sum_rows), :]
                fin[rows(h * half + at, sum_rows), :] = total
                total = total * total
                for k in range(sum_rows // 8):
                    sq = sq + total[8 * k:8 * k + 8]
                return sq
            acc[...] = lax.fori_loop(0, rc // sum_rows, body, acc[...])

    mine = rows(core * VROWS, VROWS)
    other = rows((1 - core) * VROWS, VROWS)
    vec_core = remote(vpk.at[other], vland, vs_sem.at[0], vr_sem.at[0], 1)
    vec_x = remote(vs1, vlx, vs_sem.at[1], vr_sem.at[1], 2)
    vec_y = remote(vs2, vly, vs_sem.at[2], vr_sem.at[2], 4)
    vec_back = remote(vfull.at[mine], vfull.at[mine], vs_sem.at[3], vr_sem.at[3], 1)
    vec_back_in = remote(vfull.at[other], vfull.at[other], vs_sem.at[3], vr_sem.at[3], 1)

    def vec_step(c):
        @pl.when(c == 1)
        def _():
            vraw_copy.wait()
            vpk[...] = vraw[...].astype(F32).reshape(2 * VROWS, LANES).astype(BF16)

        @pl.when(c == 2)
        def _():
            vec_core.start()

        @pl.when(c == 3)
        def _():
            vec_core.wait_recv()
            vs1[...] = vpk[mine, :].astype(F32) + vland[...].astype(F32)

        @pl.when(c == 4)
        def _():
            vec_x.start()

        @pl.when(c == 6)
        def _():
            vec_x.wait_recv()
            vs2[...] = vs1[...] + vlx[...]

        @pl.when(c == 7)
        def _():
            vec_y.start()

        @pl.when(c == 9)
        def _():
            vec_y.wait_recv()
            vfull[mine, :] = vs2[...] + vly[...]

        @pl.when(c == 10)
        def _():
            vec_back.start()

        @pl.when(c == 12)
        def _():
            vec_back_in.wait_recv()
            vec_core.wait_send()
            vec_x.wait_send()
            vec_y.wait_send()
            vec_back.wait_send()

    def scatter_step(c, _):
        @pl.when(c < NC)
        def _():
            send_chunk(c)

        @pl.when(c == 0)
        def _():
            vraw_copy.start()

        @pl.when(c == 3)
        def _():
            for copy in state_copies:
                copy.start()

        vec_step(c)

        @pl.when((c >= 1) & (c < NC + 1))
        def _():
            relay_chunk(c - 1)

        @pl.when(c >= 2)
        def _():
            final_chunk(c - 2)
        return 0

    lax.fori_loop(0, NC + 2, scatter_step, 0)

    norms[me] = acc[...]
    vec_sq = jnp.sum(vfull[...] * vfull[...], keepdims=True)
    for copy in state_copies:
        copy.wait()

    def norm_copy(mask):
        return remote(norms.at[me], norms.at[me], ns_sem.at[mask - 1], nr_sem.at[mask - 1], mask)

    for mask in (6, 7, 2, 4, 3, 5, 1):
        norm_copy(mask).start()
    for c in (NC - 2, NC - 1):
        for b in send_slot:
            block_copy(b, c).wait_send()
        for h in (0, 1):
            rel_copy(h, c).wait_send()
    for mask in range(1, N_DEV):
        norm_copy(mask).wait_recv()
    total = norms[0]
    for k in range(1, N_DEV):
        total = total + norms[k]
    norm_sq = (jnp.sum(total, keepdims=True) + vec_sq) * (1.0 / (N_DEV * N_DEV))
    clip = jnp.minimum(1.0, MAX_NORM / (jnp.sqrt(norm_sq) + NORM_EPS)) * (1.0 / N_DEV)
    lr = lr_ref[0]

    upd_rows = 32
    clip_rows = jnp.broadcast_to(clip, (upd_rows, LANES))

    def update_chunk(h, c):
        def body(i, _):
            at = h * half + c * rc + i * upd_rows
            here = rows(at, upd_rows)
            new_p, new_m, new_v = adam_update(
                fin[here, :] * clip_rows, p_ref[here, :], m_ref[here, :], v_ref[here, :], lr, WEIGHT_DECAY)
            p_ref[here, :] = new_p
            m_ref[here, :] = new_m
            v_ref[here, :] = new_v
            big[rows(me * piece_rows + at, upd_rows), :] = new_p.astype(BF16)
            return 0
        lax.fori_loop(0, rc // upd_rows, body, 0)

    def gather_copy(mask, h, c, dest, ssem, slot):
        piece = flip(me, mask) if mask else me
        ref = big.at[rows(piece * piece_rows + h * half + c * rc, rc)]
        return remote(ref, ref, ag_sem.at[ssem], rs.at[slot, c], dest)

    def own_x(h, c):
        return gather_copy(0, h, c, 2, 0, h)

    def own_y(h, c):
        return gather_copy(0, h, c, 4, 1, 2 + h)

    def own_core(h, c):
        return gather_copy(0, h, c, 1, 2, 6 + h)

    def arrived(mask, h, c, slot):
        gather_copy(mask, h, c, 1, 0, slot).wait_recv()

    def to_core(mask, h, c):
        return gather_copy(mask, h, c, 1, {2: 5, 4: 6, 6: 7}[mask], {2: 8, 4: 10, 6: 12}[mask] + h)

    def first_half(i, _):
        @pl.when(i < NC)
        def _():
            update_chunk(0, i)
            update_chunk(1, i)
            own_x(0, i).start()
            own_y(1, i).start()
            own_core(0, i).start()
            own_core(1, i).start()

        @pl.when(i >= LAG)
        def _():
            j = i - LAG
            arrived(2, 0, j, 0)
            gather_copy(2, 0, j, 4, 3, 4).start()
            to_core(2, 0, j).start()
            arrived(4, 1, j, 3)
            gather_copy(4, 1, j, 2, 4, 5).start()
            to_core(4, 1, j).start()

        @pl.when(i >= NC)
        def _():
            own_x(1, i - NC).start()
            own_y(0, i - NC).start()
        return 0

    lax.fori_loop(0, NC + LAG, first_half, 0)

    vrows = n_vec // LANES
    new_p, new_m, new_v = adam_update(
        vfull[pl.ds(0, vrows), :] * clip, pv_ref[...], mv_ref[...], vv_ref[...], lr, 0.0)
    pv_out[...] = new_p
    mv_out[...] = new_m
    vv_out[...] = new_v

    def second_half(j, _):
        @pl.when(j + LAG < NC)
        def _():
            own_x(1, j + LAG).start()
            own_y(0, j + LAG).start()
        arrived(6, 0, j, 4)
        to_core(6, 0, j).start()
        arrived(6, 1, j, 5)
        to_core(6, 1, j).start()
        arrived(2, 1, j, 1)
        to_core(2, 1, j).start()
        arrived(4, 0, j, 2)
        to_core(4, 0, j).start()
        return 0

    lax.fori_loop(0, NC, second_half, 0)

    def last_arrivals(c, _):
        for k, mask in enumerate((1, 3, 5, 7)):
            for h in (0, 1):
                arrived(mask, h, c, 6 + 2 * k + h)
        return 0

    lax.fori_loop(0, NC, last_arrivals, 0)
    for ssem, count in ((0, 2), (1, 2), (2, 2), (3, 1), (4, 1), (5, 2), (6, 2), (7, 2)):
        ref = big.at[pl.ds(0, count * half)]
        remote(ref, ref, ag_sem.at[ssem], rs.at[0, 0], 1).wait_send()
    for mask in range(1, N_DEV):
        norm_copy(mask).wait_send()


def write_kernel(splits, *refs):
    n = len(splits)
    srcs, dsts, sem = refs[:n], refs[n:2 * n], refs[2 * n]
    copies = []
    for src, dst, count in zip(srcs, dsts, splits):
        part = src.shape[0] // count
        for k in range(count):
            at = pl.ds(k * part, part)
            copies.append(pltpu.make_async_copy(src.at[at], dst.at[at], sem.at[len(copies)]))
    for copy in copies:
        copy.start()
    for copy in copies:
        copy.wait()


def solution(mesh):
    axis_name = mesh.axis_names[0]

    def local_step(g_mat, g_vec, p_mat, m_mat, v_mat, p_vec, m_vec, v_vec, learn_rate):
        n_piece = p_mat.shape[0]
        n_vec = p_vec.shape[0]
        piece_rows = n_piece // LANES
        half = piece_rows // 2
        rc = half // NC
        state = (piece_rows, LANES)
        vec = (n_vec // LANES, LANES)
        full = (N_DEV * piece_rows, LANES)
        any_spec = pl.BlockSpec(memory_space=pl.ANY)
        vmem_spec = pl.BlockSpec(memory_space=pltpu.VMEM)
        outs = pl.pallas_call(
            functools.partial(step_kernel, half, rc, n_vec),
            out_shape=[pltpu.VMEM(full, BF16)] + [pltpu.VMEM(state, F32)] * 3 + [pltpu.VMEM(vec, F32)] * 3,
            in_specs=[any_spec] * 5 + [vmem_spec] * 3 + [pl.BlockSpec(memory_space=pltpu.SMEM)],
            out_specs=[vmem_spec] * 7,
            scratch_shapes=[
                pltpu.VMEM(state, F32),
                pltpu.VMEM((NRAW, 1, rc * LANES), BF16),
                pltpu.VMEM((2, 12, rc, LANES), BF16),
                pltpu.VMEM((2, 2, rc, LANES), F32),
                pltpu.VMEM((8, LANES), F32),
                pltpu.VMEM((N_DEV, 8, LANES), F32),
                pltpu.VMEM((1, 2 * VROWS * LANES), BF16),
                pltpu.VMEM((2 * VROWS, LANES), BF16),
                pltpu.VMEM((VROWS, LANES), BF16),
                pltpu.VMEM((VROWS, LANES), F32),
                pltpu.VMEM((VROWS, LANES), F32),
                pltpu.VMEM((VROWS, LANES), F32),
                pltpu.VMEM((VROWS, LANES), F32),
                pltpu.VMEM((2 * VROWS, LANES), F32),
                pltpu.SemaphoreType.DMA((NRAW,)),
                pltpu.SemaphoreType.DMA((2, 12)),
                pltpu.SemaphoreType.DMA((2, 2)),
                pltpu.SemaphoreType.DMA((14, NC)),
                pltpu.SemaphoreType.DMA((4,)),
                pltpu.SemaphoreType.DMA((7,)),
                pltpu.SemaphoreType.DMA((7,)),
                pltpu.SemaphoreType.DMA((4,)),
                pltpu.SemaphoreType.DMA((4,)),
                pltpu.SemaphoreType.DMA((8,)),
            ],
            compiler_params=pltpu.CompilerParams(
                collective_id=0, has_side_effects=True, vmem_limit_bytes=15 * 2 ** 20),
            name="step",
        )(
            g_mat, g_vec, p_mat.reshape(state), m_mat.reshape(state), v_mat.reshape(state),
            p_vec.reshape(vec), m_vec.reshape(vec), v_vec.reshape(vec), learn_rate.reshape(1),
        )
        splits = (16, 4, 4, 4, 1, 1, 1)
        pb, p_new, m_new, v_new, pv_new, mv_new, vv_new = pl.pallas_call(
            functools.partial(write_kernel, splits),
            out_shape=[jax.ShapeDtypeStruct(o.shape, o.dtype) for o in outs],
            in_specs=[vmem_spec] * 7,
            out_specs=[any_spec] * 7,
            scratch_shapes=[pltpu.SemaphoreType.DMA((sum(splits),))],
            compiler_params=pltpu.CompilerParams(vmem_limit_bytes=2 ** 20),
            name="write",
        )(*outs)
        return (
            p_new.reshape(-1), m_new.reshape(-1), v_new.reshape(-1),
            pv_new.reshape(-1), mv_new.reshape(-1), vv_new.reshape(-1), pb.reshape(-1),
        )

    return jax.shard_map(
        local_step,
        mesh=mesh,
        in_specs=(P(axis_name, None), P(axis_name, None), P(axis_name), P(axis_name), P(axis_name), P(), P(), P(), P()),
        out_specs=(P(axis_name), P(axis_name), P(axis_name), P(), P(), P(), P()),
        check_vma=False,
    )
```

time: 1000 us -> 403 us (0.40)
  waiting for transfers between devices: 442 us -> 0 us
  Pallas kernels: 0 us -> 376 us
  other arithmetic: 273 us -> 0 us
  local copies, waits for them, and re-layouts: 230 us -> 25 us
  blocking collectives: 22.4 us -> 0 us
  between operations: 16.6 us -> 1.3 us
    pallas_call x0 -> x2, Pallas kernels: none -> 376 us  [the longest x1 360 us: local_step(): pl.pallas_call(functools.partial(step_kernel, half, rc, n_vec), out_shape...]
    all_to_all x1 -> x0, waiting for transfers between devices: 309 us -> none  [local_step(): recv_rows = lax.all_to_all(send_rows, axis_name, 0, 0, tiled=True)]
    unnamed x13 -> x8, local copies, waits for them, and re-layouts: 229 us -> 25 us
    all_to_all x1 -> x0, other arithmetic: 167 us -> none  [local_step(): recv_rows = lax.all_to_all(send_rows, axis_name, 0, 0, tiled=True)]
    all_gather x1 -> x0, waiting for transfers between devices: 133 us -> none  [local_step(): lax.all_gather(new_p_mat.astype(jnp.bfloat16), axis_name, tiled=True)]
    reduce_sum x3 -> x0, other arithmetic: 84.7 us -> none  [the longest x1 78.6 us: local_step(): grad_mat = jnp.sum(recv_rows.astype(jnp.float32), axis=0) / group_size]
    psum x1 -> x0, blocking collectives: 22.4 us -> none  [local_step(): lax.psum(jnp.sum(grad_mat * grad_mat), axis_name)]
    convert_element_type x2 -> x0, other arithmetic: 20.9 us -> none  [the longest x1 20.1 us: local_step(): new_p_mat.astype(jnp.bfloat16)]
  transfers between devices with their start and end apart: 3 -> 0, of which waited for: 2 -> 0; matrix products, arithmetic and copies ran while one was open for 15% -> 0% of each run, Pallas kernels for 0% -> 0%
where the time goes in v1:
time: 403 us; the launch traced here: 402 us
  Pallas kernels  376 us (93%)
  local copies, waits for them, and re-layouts  25 us (6%)
    pallas_call x1, Pallas kernels, local_step(): pl.pallas_call(functools.partial(step_kernel, half, rc, n_vec), out_shape...  360 us
    unnamed x8, local copies, waits for them, and re-layouts  25 us
    pallas_call x1, Pallas kernels, local_step(): pl.pallas_call(functools.partial(write_kernel, splits), out_shape=[jax.Sh...  16 us

profile of v1, /device:TPU:0, one launch (start us, length us, event | category | flops | bytes accessed | tf_op | source)
XLA Modules:
  0.0 402.1 jit_solution(2792665939715000149)
XLA Ops:
  1.3 359.8 %step.1 = (bf16[110592,128]{1,0:T(8,128)(2,1)S(1)}, f32[13824,128]{1,0:T(8,128)S(1)}, f32[13824,128]{1,0:T(8,128)S(1)}, f32[13824,128]{1,0:T(8,128)S(1)}, f32[15...) custom-call(bf16[1,14155776]{1,0:T(2,128)(2,1)} %g_hbm.1, bf16[1,19968]{1,0:T(2,128)(2,1)} %gv_hbm.1, ...), custom_call_target="tpu_custom_call" | custom-call | tf_op jit(solution)/shard_map/step/pallas_call | solution.py:443
  361.1 0.0 copy-start
  361.1 9.9 %copy-done = bf16[110592,128]{1,0:T(8,128)(2,1)} copy-done((bf16[110592,128]{1,0:T(8,128)(2,1)}, bf16[110592,128]{1,0:T(8,128)(2,1)S(1)}, u32[]{:S(2)}) %copy-start) | copy-done | bytes 28311576
  371.1 0.0 copy-start.2
  371.1 3.0 copy-done.2
  374.0 0.0 copy-start.1
  374.0 9.1 %copy-done.1 = bf16[110592,128]{1,0:T(8,128)(2,1)S(1)} copy-done((bf16[110592,128]{1,0:T(8,128)(2,1)S(1)}, bf16[110592,128]{1,0:T(8,128)(2,1)}, u32[]{:S(2)}) %copy-start.1) | copy-done | bytes 28311576
  383.1 0.0 copy-start.3
  383.1 3.0 copy-done.3
  386.1 16.0 %write.1 = (bf16[110592,128]{1,0:T(8,128)(2,1)}, f32[13824,128]{1,0:T(8,128)}, f32[13824,128]{1,0:T(8,128)}, f32[13824,128]{1,0:T(8,128)}, f32[156,128]{1,0:T(8,...) custom-call(bf16[110592,128]{1,0:T(8,128)(2,1)S(1)} %copy-done.1, f32[13824,128]{1,0:T(8,128)S(1)} %copy-done.3, ...), custom_call_target="tpu_custom_call" | custom-call | tf_op jit(solution)/shard_map/write/pallas_call | solution.py:482
Async XLA Ops:
  361.1 10.0 %copy-start = (bf16[110592,128]{1,0:T(8,128)(2,1)}, bf16[110592,128]{1,0:T(8,128)(2,1)S(1)}, u32[]{:S(2)}) copy-start(bf16[110592,128]{1,0:T(8,128)(2,1)S(1)} %get-tuple-element.21.refs_0_) | copy-start | bytes 84934656
  371.1 3.0 copy-start.2
  374.0 9.1 %copy-start.1 = (bf16[110592,128]{1,0:T(8,128)(2,1)S(1)}, bf16[110592,128]{1,0:T(8,128)(2,1)}, u32[]{:S(2)}) copy-start(bf16[110592,128]{1,0:T(8,128)(2,1)} %copy-done) | copy-start | bytes 84934656
  383.1 3.0 copy-start.3

commit v2 on v1

--- a/solution.py
+++ b/solution.py
@@ -45,11 +45,14 @@
 def step_kernel(
     half, rc, n_vec,
     g_hbm, gv_hbm, p_hbm, m_hbm, v_hbm, pv_ref, mv_ref, vv_ref, lr_ref,
-    big, p_ref, m_ref, v_ref, pv_out, mv_out, vv_out,
+    state, big,
     fin, raw, pk, rel, acc, norms, vraw, vpk, vland, vs1, vlx, vs2, vly, vfull,
     raw_sem, send_sem, rel_sem, rs, st_sem, ns_sem, nr_sem, vs_sem, vr_sem, ag_sem,
 ):
     piece_rows = 2 * half
+    p_ref, m_ref, v_ref = (state.at[pl.ds(k * piece_rows, piece_rows)] for k in range(3))
+    pv_out, mv_out, vv_out = (
+        state.at[pl.ds(3 * piece_rows + k * 2 * VROWS, n_vec // LANES)] for k in range(3))
     me = lax.axis_index("dp")
     core = lax.rem(me, 2)
     peer = {mask: flip(me, mask) for mask in range(1, N_DEV)}
@@ -411,15 +414,21 @@
         norm_copy(mask).wait_send()
 
 
-def write_kernel(splits, *refs):
-    n = len(splits)
-    srcs, dsts, sem = refs[:n], refs[n:2 * n], refs[2 * n]
+def write_kernel(state, big, *refs):
+    dsts, sem = refs[:-1], refs[-1]
     copies = []
-    for src, dst, count in zip(srcs, dsts, splits):
-        part = src.shape[0] // count
+
+    def add(src, dst, count):
+        part = dst.shape[0] // count
         for k in range(count):
-            at = pl.ds(k * part, part)
-            copies.append(pltpu.make_async_copy(src.at[at], dst.at[at], sem.at[len(copies)]))
+            copies.append(pltpu.make_async_copy(
+                src.at[pl.ds(k * part, part)], dst.at[pl.ds(k * part, part)], sem.at[len(copies)]))
+
+    at = 0
+    for dst in dsts[:6]:
+        add(state.at[pl.ds(at, dst.shape[0])], dst, 4 if dst.shape[0] > 2 * VROWS else 1)
+        at += max(dst.shape[0], 2 * VROWS)
+    add(big, dsts[6], 16)
     for copy in copies:
         copy.start()
     for copy in copies:
@@ -442,9 +451,9 @@
         vmem_spec = pl.BlockSpec(memory_space=pltpu.VMEM)
         outs = pl.pallas_call(
             functools.partial(step_kernel, half, rc, n_vec),
-            out_shape=[pltpu.VMEM(full, BF16)] + [pltpu.VMEM(state, F32)] * 3 + [pltpu.VMEM(vec, F32)] * 3,
+            out_shape=[pltpu.VMEM((3 * piece_rows + 6 * VROWS, LANES), F32), pltpu.VMEM(full, BF16)],
             in_specs=[any_spec] * 5 + [vmem_spec] * 3 + [pl.BlockSpec(memory_space=pltpu.SMEM)],
-            out_specs=[vmem_spec] * 7,
+            out_specs=[vmem_spec] * 2,
             scratch_shapes=[
                 pltpu.VMEM(state, F32),
                 pltpu.VMEM((NRAW, 1, rc * LANES), BF16),
@@ -478,13 +487,13 @@
             g_mat, g_vec, p_mat.reshape(state), m_mat.reshape(state), v_mat.reshape(state),
             p_vec.reshape(vec), m_vec.reshape(vec), v_vec.reshape(vec), learn_rate.reshape(1),
         )
-        splits = (16, 4, 4, 4, 1, 1, 1)
-        pb, p_new, m_new, v_new, pv_new, mv_new, vv_new = pl.pallas_call(
-            functools.partial(write_kernel, splits),
-            out_shape=[jax.ShapeDtypeStruct(o.shape, o.dtype) for o in outs],
-            in_specs=[vmem_spec] * 7,
+        p_new, m_new, v_new, pv_new, mv_new, vv_new, pb = pl.pallas_call(
+            write_kernel,
+            out_shape=[jax.ShapeDtypeStruct(state, F32)] * 3 + [jax.ShapeDtypeStruct(vec, F32)] * 3
+            + [jax.ShapeDtypeStruct(full, BF16)],
+            in_specs=[vmem_spec] * 2,
             out_specs=[any_spec] * 7,
-            scratch_shapes=[pltpu.SemaphoreType.DMA((sum(splits),))],
+            scratch_shapes=[pltpu.SemaphoreType.DMA((31,))],
             compiler_params=pltpu.CompilerParams(vmem_limit_bytes=2 ** 20),
             name="write",
         )(*outs)

time: 403 us -> 378 us (0.938)
  local copies, waits for them, and re-layouts: 25 us -> 0 us
    unnamed x8 -> x0, local copies, waits for them, and re-layouts: 25 us -> none
where the time goes in v2:
time: 378 us; the launch traced here: 377 us
  Pallas kernels  376 us (99%)
    pallas_call x1, Pallas kernels, local_step(): pl.pallas_call(functools.partial(step_kernel, half, rc, n_vec), out_shape...  360 us
    pallas_call x1, Pallas kernels, local_step(): pl.pallas_call(write_kernel, out_shape=[jax.ShapeDtypeStruct(state, F32)]...  16.1 us

profile of v2, /device:TPU:0, one launch (start us, length us, event | category | flops | bytes accessed | tf_op | source)
XLA Modules:
  0.0 377.2 jit_solution(4530465730747497379)
XLA Ops:
  1.3 359.8 %step.1 = (f32[41952,128]{1,0:T(8,128)S(1)}, bf16[110592,128]{1,0:T(8,128)(2,1)S(1)}) custom-call(bf16[1,14155776]{1,0:T(2,128)(2,1)} %g_hbm.1, bf16[1,19968]{1,0:T(2,128)(2,1)} %gv_hbm.1, f32[13824,128]{1,0:T(8,128)} %bitcast.15, f32[13824,128]{1,0:T(8,128)} %bitcast.16, f32[13824,128]{1,0:T(8,128)} %bitcast.17, f32[156,128]{1,0:T(8,128)} %bitcast.18, ...), custom_call_target="tpu_custom_call" | custom-call | tf_op jit(solution)/shard_map/step/pallas_call | solution.py:452
  361.1 16.1 %write.1 = (f32[13824,128]{1,0:T(8,128)}, f32[13824,128]{1,0:T(8,128)}, f32[13824,128]{1,0:T(8,128)}, f32[156,128]{1,0:T(8,128)}, f32[156,128]{1,0:T(8,128)}, /*...) custom-call(f32[41952,128]{1,0:T(8,128)S(1)} %get-tuple-element.16.state, bf16[110592,128]{1,0:T(8,128)(2,1)S(1)} %get-tuple-element.17.big), custom_call_target="tpu_custom_call" | custom-call | tf_op jit(solution)/shard_map/write/pallas_call | solution.py:490

commit v3 on v2

--- a/solution.py
+++ b/solution.py
@@ -21,6 +21,7 @@
 N_DEV = 8
 NC = 18
 NRAW = 8
+EARLY = 4
 LAG = 2
 VROWS = 80
 MESH = pl.DeviceIdType.MESH
@@ -44,9 +45,9 @@
 
 def step_kernel(
     half, rc, n_vec,
-    g_hbm, gv_hbm, p_hbm, m_hbm, v_hbm, pv_ref, mv_ref, vv_ref, lr_ref,
+    g_hbm, gv_hbm, p_hbm, m_hbm, v_hbm, pv_hbm, mv_hbm, vv_hbm, lr_hbm,
     state, big,
-    fin, raw, pk, rel, acc, norms, vraw, vpk, vland, vs1, vlx, vs2, vly, vfull,
+    fin, raw, pk, rel, acc, norms, vraw, vpk, vland, vs1, vlx, vs2, vly, vfull, lr_ref,
     raw_sem, send_sem, rel_sem, rs, st_sem, ns_sem, nr_sem, vs_sem, vr_sem, ag_sem,
 ):
     piece_rows = 2 * half
@@ -118,9 +119,11 @@
 
     state_copies = [
         pltpu.make_async_copy(src, dst, st_sem.at[i])
-        for i, (src, dst) in enumerate(((p_hbm, p_ref), (m_hbm, m_ref), (v_hbm, v_ref)))
+        for i, (src, dst) in enumerate((
+            (p_hbm, p_ref), (m_hbm, m_ref), (v_hbm, v_ref),
+            (pv_hbm, pv_out), (mv_hbm, mv_out), (vv_hbm, vv_out), (lr_hbm, lr_ref)))
     ]
-    vraw_copy = pltpu.make_async_copy(gv_hbm, vraw.at[:, pl.ds(0, n_vec)], st_sem.at[3])
+    vraw_copy = pltpu.make_async_copy(gv_hbm, vraw.at[:, pl.ds(0, n_vec)], st_sem.at[7])
 
     barrier = pltpu.get_barrier_semaphore()
     for mask in range(1, N_DEV):
@@ -130,8 +133,6 @@
     vraw[:, pl.ds(n_vec // 1024 * 1024, 2 * VROWS * LANES - n_vec // 1024 * 1024)] = jnp.zeros(
         (1, 2 * VROWS * LANES - n_vec // 1024 * 1024), BF16)
     acc[...] = jnp.zeros_like(acc)
-    pl.semaphore_wait(barrier, N_DEV - 1)
-
     step_rows = 64
 
     def pack_rows(src, dst, first):
@@ -140,26 +141,38 @@
             dst[rows(first + i * step_rows, step_rows), :] = (
                 vals.astype(F32).reshape(step_rows, LANES).astype(BF16))
             return 0
-        lax.fori_loop(0, rc // step_rows, body, 0)
+        lax.fori_loop(0, rc // step_rows, body, 0, unroll=2)
+
+    def load_block(b, c):
+        kind, _, _, _, slot = blocks[b]
+        raw_copy(b, c).wait()
+        if kind == "send":
+            @pl.when(c >= 2)
+            def _():
+                block_copy(b, c - 2).wait_send()
+            pack_rows(raw.at[b % NRAW], pk.at[lax.rem(c, 2), send_slot[b]], 0)
+        else:
+            pack_rows(raw.at[b % NRAW], big, slot * half + c * rc)
+        if b + NRAW < n_blocks:
+            raw_copy(b + NRAW, c).start()
+        else:
+            @pl.when(c + 1 < NC)
+            def _():
+                raw_copy(b + NRAW - n_blocks, c + 1).start()
+
+    for b in range(EARLY):
+        load_block(b, 0)
+    pl.semaphore_wait(barrier, N_DEV - 1)
 
     def send_chunk(c):
-        par = lax.rem(c, 2)
         waiting = None
         for b, (kind, h, mask, dest, slot) in enumerate(blocks):
-            raw_copy(b, c).wait()
-            if kind == "send":
-                @pl.when(c >= 2)
+            if b < EARLY:
+                @pl.when(c >= 1)
                 def _():
-                    block_copy(b, c - 2).wait_send()
-                pack_rows(raw.at[b % NRAW], pk.at[par, send_slot[b]], 0)
+                    load_block(b, c)
             else:
-                pack_rows(raw.at[b % NRAW], big, slot * half + c * rc)
-            if b + NRAW < n_blocks:
-                raw_copy(b + NRAW, c).start()
-            else:
-                @pl.when(c + 1 < NC)
-                def _():
-                    raw_copy(b + NRAW - n_blocks, c + 1).start()
+                load_block(b, c)
             if waiting is not None:
                 block_copy(waiting, c).start()
             waiting = b if kind == "send" else None
@@ -206,7 +219,7 @@
                 for k in range(sum_rows // 8):
                     sq = sq + total[8 * k:8 * k + 8]
                 return sq
-            acc[...] = lax.fori_loop(0, rc // sum_rows, body, acc[...])
+            acc[...] = lax.fori_loop(0, rc // sum_rows, body, acc[...], unroll=4)
 
     mine = rows(core * VROWS, VROWS)
     other = rows((1 - core) * VROWS, VROWS)
@@ -310,23 +323,24 @@
         total = total + norms[k]
     norm_sq = (jnp.sum(total, keepdims=True) + vec_sq) * (1.0 / (N_DEV * N_DEV))
     clip = jnp.minimum(1.0, MAX_NORM / (jnp.sqrt(norm_sq) + NORM_EPS)) * (1.0 / N_DEV)
-    lr = lr_ref[0]
+    lr = lr_ref[...]
 
     upd_rows = 32
     clip_rows = jnp.broadcast_to(clip, (upd_rows, LANES))
+    lr_rows = jnp.broadcast_to(lr, (upd_rows, LANES))
 
     def update_chunk(h, c):
         def body(i, _):
             at = h * half + c * rc + i * upd_rows
             here = rows(at, upd_rows)
             new_p, new_m, new_v = adam_update(
-                fin[here, :] * clip_rows, p_ref[here, :], m_ref[here, :], v_ref[here, :], lr, WEIGHT_DECAY)
+                fin[here, :] * clip_rows, p_ref[here, :], m_ref[here, :], v_ref[here, :], lr_rows, WEIGHT_DECAY)
             p_ref[here, :] = new_p
             m_ref[here, :] = new_m
             v_ref[here, :] = new_v
             big[rows(me * piece_rows + at, upd_rows), :] = new_p.astype(BF16)
             return 0
-        lax.fori_loop(0, rc // upd_rows, body, 0)
+        lax.fori_loop(0, rc // upd_rows, body, 0, unroll=4)
 
     def gather_copy(mask, h, c, dest, ssem, slot):
         piece = flip(me, mask) if mask else me
@@ -352,8 +366,8 @@
         @pl.when(i < NC)
         def _():
             update_chunk(0, i)
+            own_x(0, i).start()
             update_chunk(1, i)
-            own_x(0, i).start()
             own_y(1, i).start()
             own_core(0, i).start()
             own_core(1, i).start()
@@ -378,7 +392,7 @@
 
     vrows = n_vec // LANES
     new_p, new_m, new_v = adam_update(
-        vfull[pl.ds(0, vrows), :] * clip, pv_ref[...], mv_ref[...], vv_ref[...], lr, 0.0)
+        vfull[pl.ds(0, vrows), :] * clip, pv_out[...], mv_out[...], vv_out[...], lr, 0.0)
     pv_out[...] = new_p
     mv_out[...] = new_m
     vv_out[...] = new_v
@@ -452,7 +466,7 @@
         outs = pl.pallas_call(
             functools.partial(step_kernel, half, rc, n_vec),
             out_shape=[pltpu.VMEM((3 * piece_rows + 6 * VROWS, LANES), F32), pltpu.VMEM(full, BF16)],
-            in_specs=[any_spec] * 5 + [vmem_spec] * 3 + [pl.BlockSpec(memory_space=pltpu.SMEM)],
+            in_specs=[any_spec] * 9,
             out_specs=[vmem_spec] * 2,
             scratch_shapes=[
                 pltpu.VMEM(state, F32),
@@ -469,11 +483,12 @@
                 pltpu.VMEM((VROWS, LANES), F32),
                 pltpu.VMEM((VROWS, LANES), F32),
                 pltpu.VMEM((2 * VROWS, LANES), F32),
+                pltpu.VMEM((1, 1), F32),
                 pltpu.SemaphoreType.DMA((NRAW,)),
                 pltpu.SemaphoreType.DMA((2, 12)),
                 pltpu.SemaphoreType.DMA((2, 2)),
                 pltpu.SemaphoreType.DMA((14, NC)),
-                pltpu.SemaphoreType.DMA((4,)),
+                pltpu.SemaphoreType.DMA((8,)),
                 pltpu.SemaphoreType.DMA((7,)),
                 pltpu.SemaphoreType.DMA((7,)),
                 pltpu.SemaphoreType.DMA((4,)),
@@ -485,7 +500,7 @@
             name="step",
         )(
             g_mat, g_vec, p_mat.reshape(state), m_mat.reshape(state), v_mat.reshape(state),
-            p_vec.reshape(vec), m_vec.reshape(vec), v_vec.reshape(vec), learn_rate.reshape(1),
+            p_vec.reshape(vec), m_vec.reshape(vec), v_vec.reshape(vec), learn_rate.reshape(1, 1),
         )
         p_new, m_new, v_new, pv_new, mv_new, vv_new, pb = pl.pallas_call(
             write_kernel,

time: 378 us -> 376 us (level)
  no operation moved by 1% of the time
where the time goes in v3:
time: 376 us
  Pallas kernels  374 us (99%)
    pallas_call x1, Pallas kernels, local_step(): pl.pallas_call(functools.partial(step_kernel, half, rc, n_vec), out_shape...  358 us
    pallas_call x1, Pallas kernels, local_step(): pl.pallas_call(write_kernel, out_shape=[jax.ShapeDtypeStruct(state, F32)]...  16.1 us

profile of v3, /device:TPU:0, one launch (start us, length us, event | category | flops | bytes accessed | tf_op | source)
XLA Modules:
  0.0 375.6 jit_solution(13665678527342711419)
XLA Ops:
  1.3 358.3 %step.1 = (f32[41952,128]{1,0:T(8,128)S(1)}, bf16[110592,128]{1,0:T(8,128)(2,1)S(1)}) custom-call(bf16[1,14155776]{1,0:T(2,128)(2,1)} %g_hbm.1, bf16[1,19968]{1,0:T(2,128)(2,1)} %gv_hbm.1, f32[13824,128]{1,0:T(8,128)} %bitcast.15, f32[13824,128]{1,0:T(8,128)} %bitcast.16, f32[13824,128]{1,0:T(8,128)} %bitcast.17, f32[156,128]{1,0:T(8,128)} %bitcast.18, ...), custom_call_target="tpu_custom_call" | custom-call | tf_op jit(solution)/shard_map/step/pallas_call | solution.py:466
  359.6 16.1 %write.1 = (f32[13824,128]{1,0:T(8,128)}, f32[13824,128]{1,0:T(8,128)}, f32[13824,128]{1,0:T(8,128)}, f32[156,128]{1,0:T(8,128)}, f32[156,128]{1,0:T(8,128)}, /*...) custom-call(f32[41952,128]{1,0:T(8,128)S(1)} %get-tuple-element.16.state, bf16[110592,128]{1,0:T(8,128)(2,1)S(1)} %get-tuple-element.17.big), custom_call_target="tpu_custom_call" | custom-call | tf_op jit(solution)/shard_map/write/pallas_call | solution.py:505

commit v4 on v3

--- a/solution.py
+++ b/solution.py
@@ -22,6 +22,8 @@
 NC = 18
 NRAW = 8
 EARLY = 4
+TAIL = 6
+SPLIT = 14
 LAG = 2
 VROWS = 80
 MESH = pl.DeviceIdType.MESH
@@ -46,9 +48,9 @@
 def step_kernel(
     half, rc, n_vec,
     g_hbm, gv_hbm, p_hbm, m_hbm, v_hbm, pv_hbm, mv_hbm, vv_hbm, lr_hbm,
-    state, big,
+    state, big, px_hbm, py_hbm,
     fin, raw, pk, rel, acc, norms, vraw, vpk, vland, vs1, vlx, vs2, vly, vfull, lr_ref,
-    raw_sem, send_sem, rel_sem, rs, st_sem, ns_sem, nr_sem, vs_sem, vr_sem, ag_sem,
+    raw_sem, send_sem, rel_sem, rs, st_sem, ns_sem, nr_sem, vs_sem, vr_sem, ag_sem, px_sem,
 ):
     piece_rows = 2 * half
     p_ref, m_ref, v_ref = (state.at[pl.ds(k * piece_rows, piece_rows)] for k in range(3))
@@ -390,6 +392,15 @@
 
     lax.fori_loop(0, NC + LAG, first_half, 0)
 
+    kept = half - TAIL * rc
+    tail_copies = [
+        pltpu.make_async_copy(
+            big.at[rows(me * piece_rows + h * half + kept, TAIL * rc)], dst, px_sem.at[h])
+        for h, dst in ((1, px_hbm), (0, py_hbm))
+    ]
+    for copy in tail_copies:
+        copy.start()
+
     vrows = n_vec // LANES
     new_p, new_m, new_v = adam_update(
         vfull[pl.ds(0, vrows), :] * clip, pv_out[...], mv_out[...], vv_out[...], lr, 0.0)
@@ -398,7 +409,7 @@
     vv_out[...] = new_v
 
     def second_half(j, _):
-        @pl.when(j + LAG < NC)
+        @pl.when(j + LAG < NC - TAIL)
         def _():
             own_x(1, j + LAG).start()
             own_y(0, j + LAG).start()
@@ -406,47 +417,89 @@
         to_core(6, 0, j).start()
         arrived(6, 1, j, 5)
         to_core(6, 1, j).start()
-        arrived(2, 1, j, 1)
-        to_core(2, 1, j).start()
-        arrived(4, 0, j, 2)
-        to_core(4, 0, j).start()
+
+        @pl.when(j < NC - TAIL)
+        def _():
+            arrived(2, 1, j, 1)
+            to_core(2, 1, j).start()
+            arrived(4, 0, j, 2)
+            to_core(4, 0, j).start()
         return 0
 
     lax.fori_loop(0, NC, second_half, 0)
 
     def last_arrivals(c, _):
-        for k, mask in enumerate((1, 3, 5, 7)):
-            for h in (0, 1):
-                arrived(mask, h, c, 6 + 2 * k + h)
+        for mask, h in ((1, 0), (1, 1), (3, 0), (5, 1), (7, 0), (7, 1)):
+            arrived(mask, h, c, 5 + mask + h)
+
+        @pl.when(c < NC - TAIL)
+        def _():
+            for mask, h in ((3, 1), (5, 0)):
+                arrived(mask, h, c, 5 + mask + h)
         return 0
 
     lax.fori_loop(0, NC, last_arrivals, 0)
-    for ssem, count in ((0, 2), (1, 2), (2, 2), (3, 1), (4, 1), (5, 2), (6, 2), (7, 2)):
-        ref = big.at[pl.ds(0, count * half)]
+    for ssem, count in (
+        (0, half + kept), (1, half + kept), (2, 2 * half), (3, half), (4, half),
+        (5, half + kept), (6, half + kept), (7, 2 * half),
+    ):
+        ref = big.at[pl.ds(0, count)]
         remote(ref, ref, ag_sem.at[ssem], rs.at[0, 0], 1).wait_send()
     for mask in range(1, N_DEV):
         norm_copy(mask).wait_send()
-
-
-def write_kernel(state, big, *refs):
-    dsts, sem = refs[:-1], refs[-1]
-    copies = []
-
-    def add(src, dst, count):
-        part = dst.shape[0] // count
-        for k in range(count):
-            copies.append(pltpu.make_async_copy(
-                src.at[pl.ds(k * part, part)], dst.at[pl.ds(k * part, part)], sem.at[len(copies)]))
-
-    at = 0
-    for dst in dsts[:6]:
-        add(state.at[pl.ds(at, dst.shape[0])], dst, 4 if dst.shape[0] > 2 * VROWS else 1)
-        at += max(dst.shape[0], 2 * VROWS)
-    add(big, dsts[6], 16)
+    for copy in tail_copies:
+        copy.wait()
+
+
+def run_all(copies):
     for copy in copies:
         copy.start()
     for copy in copies:
         copy.wait()
+
+
+def first_write(half, state, big, *refs):
+    dsts, sem = refs[:-1], refs[-1]
+    copies = []
+
+    def add(src, src_at, dst, count, size):
+        part = size // count
+        for k in range(count):
+            copies.append(pltpu.make_async_copy(
+                src.at[pl.ds(src_at + k * part, part)], dst.at[pl.ds(k * part, part)], sem.at[len(copies)]))
+
+    at = 0
+    for dst in dsts[:6]:
+        size = dst.shape[0]
+        add(state, at, dst, 4 if size > 2 * VROWS else 1, size)
+        at += max(size, 2 * VROWS)
+    add(big, 0, dsts[6], SPLIT, SPLIT * half)
+    run_all(copies)
+
+
+def second_write(half, big, _, dst, sem):
+    run_all([
+        pltpu.make_async_copy(big.at[pl.ds(k * half, half)], dst.at[pl.ds(k * half, half)], sem.at[k - SPLIT])
+        for k in range(SPLIT, 2 * N_DEV)
+    ])
+
+
+def tail_write(half, tail, rx, ry, cx, cy, _, dst, buf, sem):
+    me = lax.axis_index("dp")
+    parts = ((rx, 2, 1), (ry, 4, 0), (cx, 3, 1), (cy, 5, 0))
+    fetches, stores = [], []
+    for i, (src, mask, h) in enumerate(parts):
+        at = flip(me, mask) * (2 * half) + (h + 1) * half - tail
+        fetches.append(pltpu.make_async_copy(src, buf.at[i], sem.at[i]))
+        stores.append(pltpu.make_async_copy(
+            buf.at[i], dst.at[pl.ds(pl.multiple_of(at, 16), tail)], sem.at[4 + i]))
+    for fetch in fetches:
+        fetch.start()
+    for fetch, store in zip(fetches, stores):
+        fetch.wait()
+        store.start()
+    for store in stores:
+        store.wait()
 
 
 def solution(mesh):
@@ -463,11 +516,12 @@
         full = (N_DEV * piece_rows, LANES)
         any_spec = pl.BlockSpec(memory_space=pl.ANY)
         vmem_spec = pl.BlockSpec(memory_space=pltpu.VMEM)
-        outs = pl.pallas_call(
+        state_new, big, px, py = pl.pallas_call(
             functools.partial(step_kernel, half, rc, n_vec),
-            out_shape=[pltpu.VMEM((3 * piece_rows + 6 * VROWS, LANES), F32), pltpu.VMEM(full, BF16)],
+            out_shape=[pltpu.VMEM((3 * piece_rows + 6 * VROWS, LANES), F32), pltpu.VMEM(full, BF16)]
+            + [jax.ShapeDtypeStruct((TAIL * rc, LANES), BF16)] * 2,
             in_specs=[any_spec] * 9,
-            out_specs=[vmem_spec] * 2,
+            out_specs=[vmem_spec] * 2 + [any_spec] * 2,
             scratch_shapes=[
                 pltpu.VMEM(state, F32),
                 pltpu.VMEM((NRAW, 1, rc * LANES), BF16),
@@ -494,6 +548,7 @@
                 pltpu.SemaphoreType.DMA((4,)),
                 pltpu.SemaphoreType.DMA((4,)),
                 pltpu.SemaphoreType.DMA((8,)),
+                pltpu.SemaphoreType.DMA((2,)),
             ],
             compiler_params=pltpu.CompilerParams(
                 collective_id=0, has_side_effects=True, vmem_limit_bytes=15 * 2 ** 20),
@@ -502,16 +557,47 @@
             g_mat, g_vec, p_mat.reshape(state), m_mat.reshape(state), v_mat.reshape(state),
             p_vec.reshape(vec), m_vec.reshape(vec), v_vec.reshape(vec), learn_rate.reshape(1, 1),
         )
+        def permute(values, mask):
+            return lax.ppermute(values, axis_name, [(d, d ^ mask) for d in range(N_DEV)])
+
+        def cost(n_bytes):
+            return pl.CostEstimate(flops=0, bytes_accessed=n_bytes, transcendentals=0)
+
+        rx, ry = permute(px, 2), permute(py, 4)
         p_new, m_new, v_new, pv_new, mv_new, vv_new, pb = pl.pallas_call(
-            write_kernel,
+            functools.partial(first_write, half),
             out_shape=[jax.ShapeDtypeStruct(state, F32)] * 3 + [jax.ShapeDtypeStruct(vec, F32)] * 3
             + [jax.ShapeDtypeStruct(full, BF16)],
             in_specs=[vmem_spec] * 2,
             out_specs=[any_spec] * 7,
-            scratch_shapes=[pltpu.SemaphoreType.DMA((31,))],
+            scratch_shapes=[pltpu.SemaphoreType.DMA((15 + SPLIT,))],
+            cost_estimate=cost(12 * n_piece + SPLIT * n_piece),
             compiler_params=pltpu.CompilerParams(vmem_limit_bytes=2 ** 20),
-            name="write",
-        )(*outs)
+            name="write1",
+        )(state_new, big)
+        rx, ry, p_new = lax.optimization_barrier((rx, ry, p_new))
+        cx, cy = permute(rx, 1), permute(ry, 1)
+        pb = pl.pallas_call(
+            functools.partial(second_write, half),
+            out_shape=jax.ShapeDtypeStruct(full, BF16),
+            in_specs=[vmem_spec, any_spec],
+            out_specs=any_spec,
+            input_output_aliases={1: 0},
+            scratch_shapes=[pltpu.SemaphoreType.DMA((2 * N_DEV - SPLIT,))],
+            cost_estimate=cost((2 * N_DEV - SPLIT) * n_piece),
+            compiler_params=pltpu.CompilerParams(vmem_limit_bytes=2 ** 20),
+            name="write2",
+        )(big, pb)
+        pb = pl.pallas_call(
+            functools.partial(tail_write, half, TAIL * rc),
+            out_shape=jax.ShapeDtypeStruct(full, BF16),
+            in_specs=[any_spec] * 5,
+            out_specs=any_spec,
+            input_output_aliases={4: 0},
+            scratch_shapes=[pltpu.VMEM((4, TAIL * rc, LANES), BF16), pltpu.SemaphoreType.DMA((8,))],
+            compiler_params=pltpu.CompilerParams(vmem_limit_bytes=4 * 2 ** 20),
+            name="write3",
+        )(rx, ry, cx, cy, pb)
         return (
             p_new.reshape(-1), m_new.reshape(-1), v_new.reshape(-1),
             pv_new.reshape(-1), mv_new.reshape(-1), vv_new.reshape(-1), pb.reshape(-1),

time: 376 us -> 371 us (0.987)
  Pallas kernels: 374 us -> 366 us
    pallas_call x1, Pallas kernels: 358 us -> 347 us  [local_step(): pl.pallas_call(functools.partial(step_kernel, half, rc, n_vec), out_shape...]
    pallas_call x1 -> x3, Pallas kernels: 16.1 us -> 18.7 us  [the longest x1 15 us: local_step(): pl.pallas_call(functools.partial(first_write, half), out_shape=[jax.Shape...]
  transfers between devices with their start and end apart: 0 -> 4, of which waited for: 0 -> 1; matrix products, arithmetic and copies ran while one was open for 0% -> 0% of each run, Pallas kernels for 0% -> 5%
where the time goes in v4:
time: 371 us; the launch traced here: 370 us
  Pallas kernels  366 us (99%)
    pallas_call x1, Pallas kernels, local_step(): pl.pallas_call(functools.partial(step_kernel, half, rc, n_vec), out_shape...  347 us
    pallas_call x1, Pallas kernels, local_step(): pl.pallas_call(functools.partial(first_write, half), out_shape=[jax.Shape...  15 us
  transfers between devices with their start and end apart: 4, of which 1 were waited for; matrix products, arithmetic and copies ran while one was open for 0% of the time, Pallas kernels for 5%

profile of v4, /device:TPU:0, one launch (start us, length us, event | category | flops | bytes accessed | tf_op | source)
XLA Modules:
  0.0 370.4 jit_solution(15587750088799706153)
XLA Ops:
  1.3 347.3 %step.1 = (f32[41952,128]{1,0:T(8,128)S(1)}, bf16[110592,128]{1,0:T(8,128)(2,1)S(1)}, bf16[2304,128]{1,0:T(8,128)(2,1)}, bf16[2304,128]{1,0:T(8,128)(2,1)}) custom-call(bf16[1,14155776]{1,0:T(2,128)(2,1)} %g_hbm.1, bf16[1,19968]{1,0:T(2,128)(2,1)} %gv_hbm.1, f32[13824,128]{1,0:T(8,128)} %bitcast.16, f32[13824,128]{1,0:T(8,128)} %bitcast.17, ...), custom_call_target="tpu_custom_call" | custom-call | tf_op jit(solution)/shard_map/step/pallas_call | solution.py:519
  348.6 0.7 collective-permute-start
  349.3 1.3 collective-permute-start.1
  350.6 15.0 %write1.1 = (f32[13824,128]{1,0:T(8,128)}, f32[13824,128]{1,0:T(8,128)}, f32[13824,128]{1,0:T(8,128)}, f32[156,128]{1,0:T(8,128)}, f32[156,128]{1,0:T(8,128)}, /...) custom-call(f32[41952,128]{1,0:T(8,128)S(1)} %get-tuple-element.23.state, bf16[110592,128]{1,0:T(8,128)(2,1)S(1)} %get-tuple-element.24.big), custom_call_target="tpu_custom_call" | custom-call | bytes 46006272 | tf_op jit(solution)/shard_map/write1/pallas_call | solution.py:567
  365.6 0.0 collective-permute-done.rx
  365.6 0.0 collective-permute-done.1.ry
  365.6 0.0 collective-permute-start.2
  365.7 0.5 collective-permute-start.3
  366.2 1.8 write2.1._
  368.0 0.0 collective-permute-done.2.cx
  368.0 0.5 collective-permute-done.3.cy
  368.5 1.9 write3.1
Async XLA Ops:
  348.6 17.0 %collective-permute-start = (bf16[2304,128]{1,0:T(8,128)(2,1)}, bf16[2304,128]{1,0:T(8,128)(2,1)S(1)}, u32[]{:S(2)}, u32[]{:S(2)}) collective-permute-start(bf16[2304,128]{1,0:T(8,128)(2,1)} %get-tuple-element.21), channel_id=1, source_target_pairs={{0,2},{1,3},{2,0},{3,1},{4,6},{5,7},{6,4},{7,5}} | collective-permute-start | bytes 1769480 | tf_op jit(solution)/shard_map/ppermute | solution.py:561
  349.3 16.3 %collective-permute-start.1 = (bf16[2304,128]{1,0:T(8,128)(2,1)}, bf16[2304,128]{1,0:T(8,128)(2,1)S(1)}, u32[]{:S(2)}, u32[]{:S(2)}) collective-permute-start(bf16[2304,128]{1,0:T(8,128)(2,1)} %get-tuple-element.22), channel_id=1, source_target_pairs={{0,4},{1,5},{2,6},{3,7},{4,0},{5,1},{6,2},{7,3}} | collective-permute-start | bytes 1769480 | tf_op jit(solution)/shard_map/ppermute | solution.py:561
  365.6 2.3 collective-permute-start.2
  365.7 2.8 collective-permute-start.3

commit v5 on v4

--- a/solution.py
+++ b/solution.py
@@ -22,8 +22,9 @@
 NC = 18
 NRAW = 8
 EARLY = 4
-TAIL = 6
-SPLIT = 14
+TAIL = 7
+SPLIT = 15
+DIAG_LAG = 6
 LAG = 2
 VROWS = 80
 MESH = pl.DeviceIdType.MESH
@@ -364,6 +365,12 @@
     def to_core(mask, h, c):
         return gather_copy(mask, h, c, 1, {2: 5, 4: 6, 6: 7}[mask], {2: 8, 4: 10, 6: 12}[mask] + h)
 
+    def diagonal(j):
+        arrived(6, 0, j, 4)
+        to_core(6, 0, j).start()
+        arrived(6, 1, j, 5)
+        to_core(6, 1, j).start()
+
     def first_half(i, _):
         @pl.when(i < NC)
         def _():
@@ -383,6 +390,10 @@
             arrived(4, 1, j, 3)
             gather_copy(4, 1, j, 2, 4, 5).start()
             to_core(4, 1, j).start()
+
+        @pl.when(i >= DIAG_LAG)
+        def _():
+            diagonal(i - DIAG_LAG)
 
         @pl.when(i >= NC)
         def _():
@@ -413,20 +424,16 @@
         def _():
             own_x(1, j + LAG).start()
             own_y(0, j + LAG).start()
-        arrived(6, 0, j, 4)
-        to_core(6, 0, j).start()
-        arrived(6, 1, j, 5)
-        to_core(6, 1, j).start()
-
-        @pl.when(j < NC - TAIL)
-        def _():
-            arrived(2, 1, j, 1)
-            to_core(2, 1, j).start()
-            arrived(4, 0, j, 2)
-            to_core(4, 0, j).start()
+        @pl.when(j < DIAG_LAG - LAG)
+        def _():
+            diagonal(NC + LAG - DIAG_LAG + j)
+        arrived(2, 1, j, 1)
+        to_core(2, 1, j).start()
+        arrived(4, 0, j, 2)
+        to_core(4, 0, j).start()
         return 0
 
-    lax.fori_loop(0, NC, second_half, 0)
+    lax.fori_loop(0, NC - TAIL, second_half, 0)
 
     def last_arrivals(c, _):
         for mask, h in ((1, 0), (1, 1), (3, 0), (5, 1), (7, 0), (7, 1)):
@@ -477,29 +484,30 @@
     run_all(copies)
 
 
-def second_write(half, big, _, dst, sem):
-    run_all([
-        pltpu.make_async_copy(big.at[pl.ds(k * half, half)], dst.at[pl.ds(k * half, half)], sem.at[k - SPLIT])
-        for k in range(SPLIT, 2 * N_DEV)
-    ])
-
-
-def tail_write(half, tail, rx, ry, cx, cy, _, dst, buf, sem):
+def place_tails(half, tail, parts, dst, buf, sem, others=()):
     me = lax.axis_index("dp")
-    parts = ((rx, 2, 1), (ry, 4, 0), (cx, 3, 1), (cy, 5, 0))
     fetches, stores = [], []
     for i, (src, mask, h) in enumerate(parts):
         at = flip(me, mask) * (2 * half) + (h + 1) * half - tail
         fetches.append(pltpu.make_async_copy(src, buf.at[i], sem.at[i]))
         stores.append(pltpu.make_async_copy(
-            buf.at[i], dst.at[pl.ds(pl.multiple_of(at, 16), tail)], sem.at[4 + i]))
-    for fetch in fetches:
-        fetch.start()
-    for fetch, store in zip(fetches, stores):
-        fetch.wait()
-        store.start()
-    for store in stores:
-        store.wait()
+            buf.at[i], dst.at[pl.ds(pl.multiple_of(at, 16), tail)], sem.at[2 + i]))
+    for copy in (*others, *fetches):
+        copy.start()
+    for copy in (*others, *fetches):
+        copy.wait()
+    run_all(stores)
+
+
+def second_write(half, tail, big, rx, ry, _, dst, buf, sem):
+    place_tails(half, tail, ((rx, 2, 1), (ry, 4, 0)), dst, buf, sem, [
+        pltpu.make_async_copy(big.at[pl.ds(k * half, half)], dst.at[pl.ds(k * half, half)], sem.at[4 + k - SPLIT])
+        for k in range(SPLIT, 2 * N_DEV)
+    ])
+
+
+def third_write(half, tail, cx, cy, _, dst, buf, sem):
+    place_tails(half, tail, ((cx, 3, 1), (cy, 5, 0)), dst, buf, sem)
 
 
 def solution(mesh):
@@ -577,27 +585,28 @@
         )(state_new, big)
         rx, ry, p_new = lax.optimization_barrier((rx, ry, p_new))
         cx, cy = permute(rx, 1), permute(ry, 1)
+        tail_buf = pltpu.VMEM((2, TAIL * rc, LANES), BF16)
         pb = pl.pallas_call(
-            functools.partial(second_write, half),
+            functools.partial(second_write, half, TAIL * rc),
             out_shape=jax.ShapeDtypeStruct(full, BF16),
-            in_specs=[vmem_spec, any_spec],
+            in_specs=[vmem_spec] + [any_spec] * 3,
             out_specs=any_spec,
-            input_output_aliases={1: 0},
-            scratch_shapes=[pltpu.SemaphoreType.DMA((2 * N_DEV - SPLIT,))],
+            input_output_aliases={3: 0},
+            scratch_shapes=[tail_buf, pltpu.SemaphoreType.DMA((4 + 2 * N_DEV - SPLIT,))],
             cost_estimate=cost((2 * N_DEV - SPLIT) * n_piece),
-            compiler_params=pltpu.CompilerParams(vmem_limit_bytes=2 ** 20),
+            compiler_params=pltpu.CompilerParams(vmem_limit_bytes=2 * 2 ** 20),
             name="write2",
-        )(big, pb)
+        )(big, rx, ry, pb)
         pb = pl.pallas_call(
-            functools.partial(tail_write, half, TAIL * rc),
+            functools.partial(third_write, half, TAIL * rc),
             out_shape=jax.ShapeDtypeStruct(full, BF16),
-            in_specs=[any_spec] * 5,
+            in_specs=[any_spec] * 3,
             out_specs=any_spec,
-            input_output_aliases={4: 0},
-            scratch_shapes=[pltpu.VMEM((4, TAIL * rc, LANES), BF16), pltpu.SemaphoreType.DMA((8,))],
-            compiler_params=pltpu.CompilerParams(vmem_limit_bytes=4 * 2 ** 20),
+            input_output_aliases={2: 0},
+            scratch_shapes=[tail_buf, pltpu.SemaphoreType.DMA((4,))],
+            compiler_params=pltpu.CompilerParams(vmem_limit_bytes=2 * 2 ** 20),
             name="write3",
-        )(rx, ry, cx, cy, pb)
+        )(cx, cy, pb)
         return (
             p_new.reshape(-1), m_new.reshape(-1), v_new.reshape(-1),
             pv_new.reshape(-1), mv_new.reshape(-1), vv_new.reshape(-1), pb.reshape(-1),

time: 371 us -> 368 us (level)
    pallas_call x1, Pallas kernels: 347 us -> 344 us  [local_step(): pl.pallas_call(functools.partial(step_kernel, half, rc, n_vec), out_shape...]
  transfers between devices with their start and end apart: 4 -> 4, of which waited for: 1 -> 3; matrix products, arithmetic and copies ran while one was open for 0% -> 0% of each run, Pallas kernels for 5% -> 5%
where the time goes in v5:
time: 368 us
  Pallas kernels  363 us (99%)
    pallas_call x1, Pallas kernels, local_step(): pl.pallas_call(functools.partial(step_kernel, half, rc, n_vec), out_shape...  344 us
    pallas_call x1, Pallas kernels, local_step(): pl.pallas_call(functools.partial(first_write, half), out_shape=[jax.Shape...  15.5 us
  transfers between devices with their start and end apart: 4, of which 3 were waited for; matrix products, arithmetic and copies ran while one was open for 0% of the time, Pallas kernels for 5%

profile of v5, /device:TPU:0, one launch (start us, length us, event | category | flops | bytes accessed | tf_op | source)
XLA Modules:
  0.0 367.8 jit_solution(4719675935417477185)
XLA Ops:
  1.3 343.6 %step.1 = (f32[41952,128]{1,0:T(8,128)S(1)}, bf16[110592,128]{1,0:T(8,128)(2,1)S(1)}, bf16[2688,128]{1,0:T(8,128)(2,1)}, bf16[2688,128]{1,0:T(8,128)(2,1)}) custom-call(bf16[1,14155776]{1,0:T(2,128)(2,1)} %g_hbm.1, bf16[1,19968]{1,0:T(2,128)(2,1)} %gv_hbm.1, f32[13824,128]{1,0:T(8,128)} %bitcast.16, f32[13824,128]{1,0:T(8,128)} %bitcast.17, ...), custom_call_target="tpu_custom_call" | custom-call | tf_op jit(solution)/shard_map/step/pallas_call | solution.py:527
  344.8 0.7 collective-permute-start
  345.5 1.3 collective-permute-start.1
  346.8 15.5 %write1.1 = (f32[13824,128]{1,0:T(8,128)}, f32[13824,128]{1,0:T(8,128)}, f32[13824,128]{1,0:T(8,128)}, f32[156,128]{1,0:T(8,128)}, f32[156,128]{1,0:T(8,128)}, /...) custom-call(f32[41952,128]{1,0:T(8,128)S(1)} %get-tuple-element.23.state, bf16[110592,128]{1,0:T(8,128)(2,1)S(1)} %get-tuple-element.24.big), custom_call_target="tpu_custom_call" | custom-call | bytes 47775744 | tf_op jit(solution)/shard_map/write1/pallas_call | solution.py:575
  362.3 0.3 collective-permute-done.rx
  362.7 0.4 collective-permute-done.1.ry
  363.0 0.0 collective-permute-start.2
  363.0 0.5 collective-permute-start.3
  363.5 2.3 write2.1._
  365.9 0.0 collective-permute-done.2.cx
  365.9 0.3 collective-permute-done.3.cy
  366.2 1.6 write3.1
Async XLA Ops:
  344.8 17.8 %collective-permute-start = (bf16[2688,128]{1,0:T(8,128)(2,1)}, bf16[2688,128]{1,0:T(8,128)(2,1)S(1)}, u32[]{:S(2)}, u32[]{:S(2)}) collective-permute-start(bf16[2688,128]{1,0:T(8,128)(2,1)} %get-tuple-element.21), channel_id=1, source_target_pairs={{0,2},{1,3},{2,0},{3,1},{4,6},{5,7},{6,4},{7,5}} | collective-permute-start | bytes 2064392 | tf_op jit(solution)/shard_map/ppermute | solution.py:569
  345.5 17.5 %collective-permute-start.1 = (bf16[2688,128]{1,0:T(8,128)(2,1)}, bf16[2688,128]{1,0:T(8,128)(2,1)S(1)}, u32[]{:S(2)}, u32[]{:S(2)}) collective-permute-start(bf16[2688,128]{1,0:T(8,128)(2,1)} %get-tuple-element.22), channel_id=1, source_target_pairs={{0,4},{1,5},{2,6},{3,7},{4,0},{5,1},{6,2},{7,3}} | collective-permute-start | bytes 2064392 | tf_op jit(solution)/shard_map/ppermute | solution.py:569
  363.0 2.8 collective-permute-start.2
  363.0 3.1 collective-permute-start.3

commit v6 on v5

--- a/solution.py
+++ b/solution.py
@@ -22,6 +22,7 @@
 NC = 18
 NRAW = 8
 EARLY = 4
+FIRST_PARTS = 3
 TAIL = 7
 SPLIT = 15
 DIAG_LAG = 6
@@ -216,7 +217,7 @@
                 total = big[rows((12 + h) * half + at, sum_rows), :].astype(F32)
                 for j in (2, 0, 1):
                     total = total + big[rows((6 + h * 3 + j) * half + at, sum_rows), :].astype(F32)
-                total = total + fin[rows(h * half + at, sum_rows), :]
+                total = (total + fin[rows(h * half + at, sum_rows), :]) * (1.0 / N_DEV)
                 fin[rows(h * half + at, sum_rows), :] = total
                 total = total * total
                 for k in range(sum_rows // 8):
@@ -263,7 +264,7 @@
         @pl.when(c == 9)
         def _():
             vec_y.wait_recv()
-            vfull[mine, :] = vs2[...] + vly[...]
+            vfull[mine, :] = (vs2[...] + vly[...]) * (1.0 / N_DEV)
 
         @pl.when(c == 10)
         def _():
@@ -324,17 +325,17 @@
     total = norms[0]
     for k in range(1, N_DEV):
         total = total + norms[k]
-    norm_sq = (jnp.sum(total, keepdims=True) + vec_sq) * (1.0 / (N_DEV * N_DEV))
-    clip = jnp.minimum(1.0, MAX_NORM / (jnp.sqrt(norm_sq) + NORM_EPS)) * (1.0 / N_DEV)
+    norm_sq = jnp.sum(total, keepdims=True) + vec_sq
+    clip = jnp.minimum(1.0, MAX_NORM / (jnp.sqrt(norm_sq) + NORM_EPS))
     lr = lr_ref[...]
 
     upd_rows = 32
     clip_rows = jnp.broadcast_to(clip, (upd_rows, LANES))
     lr_rows = jnp.broadcast_to(lr, (upd_rows, LANES))
 
-    def update_chunk(h, c):
+    def update_chunk(h, c, first=0, count=rc):
         def body(i, _):
-            at = h * half + c * rc + i * upd_rows
+            at = h * half + c * rc + first + i * upd_rows
             here = rows(at, upd_rows)
             new_p, new_m, new_v = adam_update(
                 fin[here, :] * clip_rows, p_ref[here, :], m_ref[here, :], v_ref[here, :], lr_rows, WEIGHT_DECAY)
@@ -343,7 +344,7 @@
             v_ref[here, :] = new_v
             big[rows(me * piece_rows + at, upd_rows), :] = new_p.astype(BF16)
             return 0
-        lax.fori_loop(0, rc // upd_rows, body, 0, unroll=4)
+        lax.fori_loop(0, count // upd_rows, body, 0, unroll=4)
 
     def gather_copy(mask, h, c, dest, ssem, slot):
         piece = flip(me, mask) if mask else me
@@ -374,10 +375,12 @@
     def first_half(i, _):
         @pl.when(i < NC)
         def _():
-            update_chunk(0, i)
-            own_x(0, i).start()
-            update_chunk(1, i)
-            own_y(1, i).start()
+            @pl.when(i > 0)
+            def _():
+                update_chunk(0, i)
+                own_x(0, i).start()
+                update_chunk(1, i)
+                own_y(1, i).start()
             own_core(0, i).start()
             own_core(1, i).start()
 
@@ -401,6 +404,12 @@
             own_y(0, i - NC).start()
         return 0
 
+    for k in range(FIRST_PARTS):
+        part = rc // FIRST_PARTS
+        for h, dest, ssem in ((0, 2, 0), (1, 4, 1)):
+            update_chunk(h, 0, k * part, part)
+            ref = big.at[rows(me * piece_rows + h * half + k * part, part)]
+            remote(ref, ref, ag_sem.at[ssem], rs.at[3 * h, 0], dest).start()
     lax.fori_loop(0, NC + LAG, first_half, 0)
 
     kept = half - TAIL * rc
@@ -484,30 +493,26 @@
     run_all(copies)
 
 
-def place_tails(half, tail, parts, dst, buf, sem, others=()):
+def tail_copies_of(half, parts, dst, sem):
     me = lax.axis_index("dp")
-    fetches, stores = [], []
+    copies = []
     for i, (src, mask, h) in enumerate(parts):
+        tail = src.shape[0]
         at = flip(me, mask) * (2 * half) + (h + 1) * half - tail
-        fetches.append(pltpu.make_async_copy(src, buf.at[i], sem.at[i]))
-        stores.append(pltpu.make_async_copy(
-            buf.at[i], dst.at[pl.ds(pl.multiple_of(at, 16), tail)], sem.at[2 + i]))
-    for copy in (*others, *fetches):
-        copy.start()
-    for copy in (*others, *fetches):
-        copy.wait()
-    run_all(stores)
-
-
-def second_write(half, tail, big, rx, ry, _, dst, buf, sem):
-    place_tails(half, tail, ((rx, 2, 1), (ry, 4, 0)), dst, buf, sem, [
-        pltpu.make_async_copy(big.at[pl.ds(k * half, half)], dst.at[pl.ds(k * half, half)], sem.at[4 + k - SPLIT])
+        copies.append(pltpu.make_async_copy(src, dst.at[pl.ds(pl.multiple_of(at, 16), tail)], sem.at[i]))
+    return copies
+
+
+def second_write(half, big, rx, ry, _, dst, sem):
+    run_all([
+        pltpu.make_async_copy(big.at[pl.ds(k * half, half)], dst.at[pl.ds(k * half, half)], sem.at[2 + k - SPLIT])
         for k in range(SPLIT, 2 * N_DEV)
     ])
-
-
-def third_write(half, tail, cx, cy, _, dst, buf, sem):
-    place_tails(half, tail, ((cx, 3, 1), (cy, 5, 0)), dst, buf, sem)
+    run_all(tail_copies_of(half, ((rx, 2, 1), (ry, 4, 0)), dst, sem))
+
+
+def third_write(half, cx, cy, _, dst, sem):
+    run_all(tail_copies_of(half, ((cx, 3, 1), (cy, 5, 0)), dst, sem))
 
 
 def solution(mesh):
@@ -585,25 +590,24 @@
         )(state_new, big)
         rx, ry, p_new = lax.optimization_barrier((rx, ry, p_new))
         cx, cy = permute(rx, 1), permute(ry, 1)
-        tail_buf = pltpu.VMEM((2, TAIL * rc, LANES), BF16)
         pb = pl.pallas_call(
-            functools.partial(second_write, half, TAIL * rc),
+            functools.partial(second_write, half),
             out_shape=jax.ShapeDtypeStruct(full, BF16),
-            in_specs=[vmem_spec] + [any_spec] * 3,
+            in_specs=[vmem_spec] * 3 + [any_spec],
             out_specs=any_spec,
             input_output_aliases={3: 0},
-            scratch_shapes=[tail_buf, pltpu.SemaphoreType.DMA((4 + 2 * N_DEV - SPLIT,))],
+            scratch_shapes=[pltpu.SemaphoreType.DMA((2 + 2 * N_DEV - SPLIT,))],
             cost_estimate=cost((2 * N_DEV - SPLIT) * n_piece),
             compiler_params=pltpu.CompilerParams(vmem_limit_bytes=2 * 2 ** 20),
             name="write2",
         )(big, rx, ry, pb)
         pb = pl.pallas_call(
-            functools.partial(third_write, half, TAIL * rc),
+            functools.partial(third_write, half),
             out_shape=jax.ShapeDtypeStruct(full, BF16),
-            in_specs=[any_spec] * 3,
+            in_specs=[vmem_spec] * 2 + [any_spec],
             out_specs=any_spec,
             input_output_aliases={2: 0},
-            scratch_shapes=[tail_buf, pltpu.SemaphoreType.DMA((4,))],
+            scratch_shapes=[pltpu.SemaphoreType.DMA((2,))],
             compiler_params=pltpu.CompilerParams(vmem_limit_bytes=2 * 2 ** 20),
             name="write3",
         )(cx, cy, pb)

time: 368 us -> 368 us (level)
  no operation moved by 1% of the time
where the time goes in v6:
time: 368 us; the launch traced here: 367 us
  Pallas kernels  362 us (98%)
    pallas_call x1, Pallas kernels, local_step(): pl.pallas_call(functools.partial(step_kernel, half, rc, n_vec), out_shape...  343 us
    pallas_call x1, Pallas kernels, local_step(): pl.pallas_call(functools.partial(first_write, half), out_shape=[jax.Shape...  15.5 us
  transfers between devices with their start and end apart: 4, of which 3 were waited for; matrix products, arithmetic and copies ran while one was open for 0% of the time, Pallas kernels for 5%

profile of v6, /device:TPU:0, one launch (start us, length us, event | category | flops | bytes accessed | tf_op | source)
XLA Modules:
  0.0 367.1 jit_solution(3204704361813408954)
XLA Ops:
  1.3 343.3 %step.1 = (f32[41952,128]{1,0:T(8,128)S(1)}, bf16[110592,128]{1,0:T(8,128)(2,1)S(1)}, bf16[2688,128]{1,0:T(8,128)(2,1)}, bf16[2688,128]{1,0:T(8,128)(2,1)}) custom-call(bf16[1,14155776]{1,0:T(2,128)(2,1)} %g_hbm.1, bf16[1,19968]{1,0:T(2,128)(2,1)} %gv_hbm.1, f32[13824,128]{1,0:T(8,128)} %bitcast.16, f32[13824,128]{1,0:T(8,128)} %bitcast.17, ...), custom_call_target="tpu_custom_call" | custom-call | tf_op jit(solution)/shard_map/step/pallas_call | solution.py:532
  344.6 0.7 collective-permute-start
  345.3 1.4 collective-permute-start.1
  346.7 15.5 %write1.1 = (f32[13824,128]{1,0:T(8,128)}, f32[13824,128]{1,0:T(8,128)}, f32[13824,128]{1,0:T(8,128)}, f32[156,128]{1,0:T(8,128)}, f32[156,128]{1,0:T(8,128)}, /...) custom-call(f32[41952,128]{1,0:T(8,128)S(1)} %get-tuple-element.23.state, bf16[110592,128]{1,0:T(8,128)(2,1)S(1)} %get-tuple-element.24.big), custom_call_target="tpu_custom_call" | custom-call | bytes 47775744 | tf_op jit(solution)/shard_map/write1/pallas_call | solution.py:580
  362.2 0.2 collective-permute-done.rx
  362.4 0.5 collective-permute-done.1.ry
  362.8 0.0 collective-permute-start.2
  362.8 0.5 collective-permute-start.3
  363.3 2.3 write2.1._
  365.7 0.0 collective-permute-done.2.cx
  365.7 0.3 collective-permute-done.3.cy
  366.0 1.1 write3.1
Async XLA Ops:
  344.6 17.8 %collective-permute-start = (bf16[2688,128]{1,0:T(8,128)(2,1)}, bf16[2688,128]{1,0:T(8,128)(2,1)S(1)}, u32[]{:S(2)}, u32[]{:S(2)}) collective-permute-start(bf16[2688,128]{1,0:T(8,128)(2,1)} %get-tuple-element.21), channel_id=1, source_target_pairs={{0,2},{1,3},{2,0},{3,1},{4,6},{5,7},{6,4},{7,5}} | collective-permute-start | bytes 2064392 | tf_op jit(solution)/shard_map/ppermute | solution.py:574
  345.3 17.5 %collective-permute-start.1 = (bf16[2688,128]{1,0:T(8,128)(2,1)}, bf16[2688,128]{1,0:T(8,128)(2,1)S(1)}, u32[]{:S(2)}, u32[]{:S(2)}) collective-permute-start(bf16[2688,128]{1,0:T(8,128)(2,1)} %get-tuple-element.22), channel_id=1, source_target_pairs={{0,4},{1,5},{2,6},{3,7},{4,0},{5,1},{6,2},{7,3}} | collective-permute-start | bytes 2064392 | tf_op jit(solution)/shard_map/ppermute | solution.py:574
  362.8 2.8 collective-permute-start.2
  362.8 3.1 collective-permute-start.3

commit v7 on v6

--- a/solution.py
+++ b/solution.py
@@ -19,13 +19,13 @@
 
 LANES = 128
 N_DEV = 8
-NC = 18
+NC = 12
 NRAW = 8
 EARLY = 4
-FIRST_PARTS = 3
-TAIL = 7
+FIRST_PARTS = 6
+TAIL = 5
 SPLIT = 15
-DIAG_LAG = 6
+DIAG_LAG = 4
 LAG = 2
 VROWS = 80
 MESH = pl.DeviceIdType.MESH
@@ -202,7 +202,7 @@
                     total = total + big[rows((h * 3 + j) * half + at, sum_rows), :].astype(F32)
                 rel[par, h, rows(i * sum_rows, sum_rows), :] = total
                 return 0
-            lax.fori_loop(0, rc // sum_rows, body, 0)
+            lax.fori_loop(0, rc // sum_rows, body, 0, unroll=3)
         for h in (0, 1):
             rel_copy(h, c).start()
 
@@ -223,7 +223,7 @@
                 for k in range(sum_rows // 8):
                     sq = sq + total[8 * k:8 * k + 8]
                 return sq
-            acc[...] = lax.fori_loop(0, rc // sum_rows, body, acc[...], unroll=4)
+            acc[...] = lax.fori_loop(0, rc // sum_rows, body, acc[...], unroll=6)
 
     mine = rows(core * VROWS, VROWS)
     other = rows((1 - core) * VROWS, VROWS)
@@ -344,7 +344,7 @@
             v_ref[here, :] = new_v
             big[rows(me * piece_rows + at, upd_rows), :] = new_p.astype(BF16)
             return 0
-        lax.fori_loop(0, count // upd_rows, body, 0, unroll=4)
+        lax.fori_loop(0, count // upd_rows, body, 0, unroll=3)
 
     def gather_copy(mask, h, c, dest, ssem, slot):
         piece = flip(me, mask) if mask else me

time: 368 us -> 367 us (level)
  no operation moved by 1% of the time
where the time goes in v7:
time: 367 us
  Pallas kernels  361 us (98%)
    pallas_call x1, Pallas kernels, local_step(): pl.pallas_call(functools.partial(step_kernel, half, rc, n_vec), out_shape...  342 us
    pallas_call x1, Pallas kernels, local_step(): pl.pallas_call(functools.partial(first_write, half), out_shape=[jax.Shape...  15.5 us
  transfers between devices with their start and end apart: 4, of which 3 were waited for; matrix products, arithmetic and copies ran while one was open for 0% of the time, Pallas kernels for 5%

profile of v7, /device:TPU:0, one launch (start us, length us, event | category | flops | bytes accessed | tf_op | source)
XLA Modules:
  0.0 366.6 jit_solution(16490611345830733642)
XLA Ops:
  1.3 341.6 %step.1 = (f32[41952,128]{1,0:T(8,128)S(1)}, bf16[110592,128]{1,0:T(8,128)(2,1)S(1)}, bf16[2880,128]{1,0:T(8,128)(2,1)}, bf16[2880,128]{1,0:T(8,128)(2,1)}) custom-call(bf16[1,14155776]{1,0:T(2,128)(2,1)} %g_hbm.1, bf16[1,19968]{1,0:T(2,128)(2,1)} %gv_hbm.1, f32[13824,128]{1,0:T(8,128)} %bitcast.16, f32[13824,128]{1,0:T(8,128)} %bitcast.17, ...), custom_call_target="tpu_custom_call" | custom-call | tf_op jit(solution)/shard_map/step/pallas_call | solution.py:532
  342.9 0.8 collective-permute-start
  343.7 1.4 collective-permute-start.1
  345.1 15.5 %write1.1 = (f32[13824,128]{1,0:T(8,128)}, f32[13824,128]{1,0:T(8,128)}, f32[13824,128]{1,0:T(8,128)}, f32[156,128]{1,0:T(8,128)}, f32[156,128]{1,0:T(8,128)}, /...) custom-call(f32[41952,128]{1,0:T(8,128)S(1)} %get-tuple-element.23.state, bf16[110592,128]{1,0:T(8,128)(2,1)S(1)} %get-tuple-element.24.big), custom_call_target="tpu_custom_call" | custom-call | bytes 47775744 | tf_op jit(solution)/shard_map/write1/pallas_call | solution.py:580
  360.6 1.1 collective-permute-done.rx
  361.7 0.5 collective-permute-done.1.ry
  362.2 0.0 collective-permute-start.2
  362.3 0.5 collective-permute-start.3
  362.8 2.3 write2.1._
  365.1 0.0 collective-permute-done.2.cx
  365.1 0.4 collective-permute-done.3.cy
  365.5 1.1 write3.1
Async XLA Ops:
  342.9 18.9 %collective-permute-start = (bf16[2880,128]{1,0:T(8,128)(2,1)}, bf16[2880,128]{1,0:T(8,128)(2,1)S(1)}, u32[]{:S(2)}, u32[]{:S(2)}) collective-permute-start(bf16[2880,128]{1,0:T(8,128)(2,1)} %get-tuple-element.21), channel_id=1, source_target_pairs={{0,2},{1,3},{2,0},{3,1},{4,6},{5,7},{6,4},{7,5}} | collective-permute-start | bytes 2211848 | tf_op jit(solution)/shard_map/ppermute | solution.py:574
  343.7 18.6 %collective-permute-start.1 = (bf16[2880,128]{1,0:T(8,128)(2,1)}, bf16[2880,128]{1,0:T(8,128)(2,1)S(1)}, u32[]{:S(2)}, u32[]{:S(2)}) collective-permute-start(bf16[2880,128]{1,0:T(8,128)(2,1)} %get-tuple-element.22), channel_id=1, source_target_pairs={{0,4},{1,5},{2,6},{3,7},{4,0},{5,1},{6,2},{7,3}} | collective-permute-start | bytes 2211848 | tf_op jit(solution)/shard_map/ppermute | solution.py:574
  362.2 2.9 collective-permute-start.2
  362.3 3.3 collective-permute-start.3

commit v8 on v7

--- a/solution.py
+++ b/solution.py
@@ -190,6 +190,8 @@
         for h in (0, 1):
             for j in range(3):
                 landed(h * 3 + j, c).wait_recv()
+            if h == 1:
+                rel_copy(0, c).start()
 
             @pl.when(c >= 2)
             def _():
@@ -203,8 +205,7 @@
                 rel[par, h, rows(i * sum_rows, sum_rows), :] = total
                 return 0
             lax.fori_loop(0, rc // sum_rows, body, 0, unroll=3)
-        for h in (0, 1):
-            rel_copy(h, c).start()
+        rel_copy(1, c).start()
 
     def final_chunk(c):
         for h in (0, 1):

time: 367 us -> 367 us (level)
  no operation moved by 1% of the time
where the time goes in v8:
time: 367 us
  Pallas kernels  361 us (98%)
    pallas_call x1, Pallas kernels, local_step(): pl.pallas_call(functools.partial(step_kernel, half, rc, n_vec), out_shape...  342 us
    pallas_call x1, Pallas kernels, local_step(): pl.pallas_call(functools.partial(first_write, half), out_shape=[jax.Shape...  15.5 us
  transfers between devices with their start and end apart: 4, of which 3 were waited for; matrix products, arithmetic and copies ran while one was open for 0% of the time, Pallas kernels for 5%

profile of v8, /device:TPU:0, one launch (start us, length us, event | category | flops | bytes accessed | tf_op | source)
XLA Modules:
  0.0 366.6 jit_solution(8552058369917538698)
XLA Ops:
  1.3 341.6 %step.1 = (f32[41952,128]{1,0:T(8,128)S(1)}, bf16[110592,128]{1,0:T(8,128)(2,1)S(1)}, bf16[2880,128]{1,0:T(8,128)(2,1)}, bf16[2880,128]{1,0:T(8,128)(2,1)}) custom-call(bf16[1,14155776]{1,0:T(2,128)(2,1)} %g_hbm.1, bf16[1,19968]{1,0:T(2,128)(2,1)} %gv_hbm.1, f32[13824,128]{1,0:T(8,128)} %bitcast.16, f32[13824,128]{1,0:T(8,128)} %bitcast.17, ...), custom_call_target="tpu_custom_call" | custom-call | tf_op jit(solution)/shard_map/step/pallas_call | solution.py:533
  342.9 0.8 collective-permute-start
  343.7 1.4 collective-permute-start.1
  345.1 15.5 %write1.1 = (f32[13824,128]{1,0:T(8,128)}, f32[13824,128]{1,0:T(8,128)}, f32[13824,128]{1,0:T(8,128)}, f32[156,128]{1,0:T(8,128)}, f32[156,128]{1,0:T(8,128)}, /...) custom-call(f32[41952,128]{1,0:T(8,128)S(1)} %get-tuple-element.23.state, bf16[110592,128]{1,0:T(8,128)(2,1)S(1)} %get-tuple-element.24.big), custom_call_target="tpu_custom_call" | custom-call | bytes 47775744 | tf_op jit(solution)/shard_map/write1/pallas_call | solution.py:581
  360.6 1.1 collective-permute-done.rx
  361.7 0.5 collective-permute-done.1.ry
  362.2 0.0 collective-permute-start.2
  362.3 0.5 collective-permute-start.3
  362.8 2.3 write2.1._
  365.1 0.0 collective-permute-done.2.cx
  365.1 0.4 collective-permute-done.3.cy
  365.5 1.1 write3.1
Async XLA Ops:
  342.9 18.9 %collective-permute-start = (bf16[2880,128]{1,0:T(8,128)(2,1)}, bf16[2880,128]{1,0:T(8,128)(2,1)S(1)}, u32[]{:S(2)}, u32[]{:S(2)}) collective-permute-start(bf16[2880,128]{1,0:T(8,128)(2,1)} %get-tuple-element.21), channel_id=1, source_target_pairs={{0,2},{1,3},{2,0},{3,1},{4,6},{5,7},{6,4},{7,5}} | collective-permute-start | bytes 2211848 | tf_op jit(solution)/shard_map/ppermute | solution.py:575
  343.7 18.6 %collective-permute-start.1 = (bf16[2880,128]{1,0:T(8,128)(2,1)}, bf16[2880,128]{1,0:T(8,128)(2,1)S(1)}, u32[]{:S(2)}, u32[]{:S(2)}) collective-permute-start(bf16[2880,128]{1,0:T(8,128)(2,1)} %get-tuple-element.22), channel_id=1, source_target_pairs={{0,4},{1,5},{2,6},{3,7},{4,0},{5,1},{6,2},{7,3}} | collective-permute-start | bytes 2211848 | tf_op jit(solution)/shard_map/ppermute | solution.py:575
  362.2 2.9 collective-permute-start.2
  362.3 3.3 collective-permute-start.3

commit v9 on v7

--- a/solution.py
+++ b/solution.py
@@ -24,7 +24,7 @@
 EARLY = 4
 FIRST_PARTS = 6
 TAIL = 5
-SPLIT = 15
+SPLIT = 16
 DIAG_LAG = 4
 LAG = 2
 VROWS = 80

time: 367 us -> 367 us (level)
  transfers between devices with their start and end apart: 4 -> 4, of which waited for: 3 -> 4; matrix products, arithmetic and copies ran while one was open for 0% -> 0% of each run, Pallas kernels for 5% -> 5%
where the time goes in v9:
time: 367 us
  Pallas kernels  360 us (98%)
    pallas_call x1, Pallas kernels, local_step(): pl.pallas_call(functools.partial(step_kernel, half, rc, n_vec), out_shape...  342 us
    pallas_call x1, Pallas kernels, local_step(): pl.pallas_call(functools.partial(first_write, half), out_shape=[jax.Shape...  16.1 us
  transfers between devices with their start and end apart: 4, of which 4 were waited for; matrix products, arithmetic and copies ran while one was open for 0% of the time, Pallas kernels for 5%

profile of v9, /device:TPU:0, one launch (start us, length us, event | category | flops | bytes accessed | tf_op | source)
XLA Modules:
  0.0 366.6 jit_solution(18070768904647628182)
XLA Ops:
  1.3 341.6 %step.1 = (f32[41952,128]{1,0:T(8,128)S(1)}, bf16[110592,128]{1,0:T(8,128)(2,1)S(1)}, bf16[2880,128]{1,0:T(8,128)(2,1)}, bf16[2880,128]{1,0:T(8,128)(2,1)}) custom-call(bf16[1,14155776]{1,0:T(2,128)(2,1)} %g_hbm.1, bf16[1,19968]{1,0:T(2,128)(2,1)} %gv_hbm.1, f32[13824,128]{1,0:T(8,128)} %bitcast.16, f32[13824,128]{1,0:T(8,128)} %bitcast.17, ...), custom_call_target="tpu_custom_call" | custom-call | tf_op jit(solution)/shard_map/step/pallas_call | solution.py:532
  342.9 0.8 collective-permute-start
  343.7 1.4 collective-permute-start.1
  345.1 16.1 %write1.1 = (f32[13824,128]{1,0:T(8,128)}, f32[13824,128]{1,0:T(8,128)}, f32[13824,128]{1,0:T(8,128)}, f32[156,128]{1,0:T(8,128)}, f32[156,128]{1,0:T(8,128)}, /...) custom-call(f32[41952,128]{1,0:T(8,128)S(1)} %get-tuple-element.23.state, bf16[110592,128]{1,0:T(8,128)(2,1)S(1)} %get-tuple-element.24.big), custom_call_target="tpu_custom_call" | custom-call | bytes 49545216 | tf_op jit(solution)/shard_map/write1/pallas_call | solution.py:580
  361.1 0.6 collective-permute-done.rx
  361.7 0.5 collective-permute-done.1.ry
  362.2 0.0 collective-permute-start.2
  362.3 0.5 collective-permute-start.3
  362.8 1.1 write2.1._
  363.9 0.6 collective-permute-done.2.cx
  364.5 1.1 collective-permute-done.3.cy
  365.5 1.1 write3.1
Async XLA Ops:
  342.9 18.9 %collective-permute-start = (bf16[2880,128]{1,0:T(8,128)(2,1)}, bf16[2880,128]{1,0:T(8,128)(2,1)S(1)}, u32[]{:S(2)}, u32[]{:S(2)}) collective-permute-start(bf16[2880,128]{1,0:T(8,128)(2,1)} %get-tuple-element.21), channel_id=1, source_target_pairs={{0,2},{1,3},{2,0},{3,1},{4,6},{5,7},{6,4},{7,5}} | collective-permute-start | bytes 2211848 | tf_op jit(solution)/shard_map/ppermute | solution.py:574
  343.7 18.6 %collective-permute-start.1 = (bf16[2880,128]{1,0:T(8,128)(2,1)}, bf16[2880,128]{1,0:T(8,128)(2,1)S(1)}, u32[]{:S(2)}, u32[]{:S(2)}) collective-permute-start(bf16[2880,128]{1,0:T(8,128)(2,1)} %get-tuple-element.22), channel_id=1, source_target_pairs={{0,4},{1,5},{2,6},{3,7},{4,0},{5,1},{6,2},{7,3}} | collective-permute-start | bytes 2211848 | tf_op jit(solution)/shard_map/ppermute | solution.py:574
  362.2 2.2 collective-permute-start.2
  362.3 3.3 collective-permute-start.3
